TPU v7x, 512 devices: a whole 4x8x8 slice. The times are simulated.
512 devices in a mesh: gx: 8 (over z), gy: 4 (over x), gz: 16 (over y, core).
Axes of the slice: x: 4, y: 8, z: 8, core: 2. Of those that a mesh axis runs over, the one named last changes fastest.
Arguments:
- right_side: float32 [64, 64, 2048], P('gx', 'gy', 'gz'), may hold values from -40 to 40
- fiber_class: int32 [64, 64, 2048], P('gx', 'gy', 'gz'), may hold values from 0 to 15
- conductivity_scale: float32 [64, 64, 2048], P('gx', 'gy', 'gz'), may hold values from 0.8 to 1.25
- class_tensor: float32 [6, 16], replicated, may hold values from -0.15 to 1.8, as said below
- block_ids: int32 [8, 4, 32], replicated, may hold values from 0 to 63, as said below
Outputs:
- solution: float32 [64, 64, 2048], P('gx', 'gy', 'gz')
- residual: float32 [64, 64, 2048], P('gx', 'gy', 'gz')
Inputs may be any that keep to these rules, and one draw needn't show every extreme that they name: `class_tensor`: column k is the tensor t I + (l - t) f f^T for a unit vector f, with 1 <= t <= 1.5 and 1.05 <= l / t <= 1.2. `block_ids`: each subdomain number names exactly 16 blocks.
All inputs are finite; a program needn't handle non-finite values.
Results may differ from a plain program's by a relative error of at most 0.0003.
Values sent between devices are 32-bit elements; how exact they have to be, the bound alone decides.
No kernel may reach another device: no remote copies, remote signals or barrier semaphores. Data moves between devices by JAX's collectives and lax.ppermute only.
A program may use at most 64 MiB of HBM per device.

v0:
```python
import functools

import jax
import jax.numpy as jnp
from jax import lax
from jax.sharding import Mesh
from jax.sharding import PartitionSpec as P

CX = 8
CY = 16
CZ = 128
ZBLK = 2
BZ = 64
COARSE = 64
NCLS = 16
ITERS = 2
GX_GY_GZ = ("gx", "gy", "gz_0", "gz_1")
GZ = ("gz_0", "gz_1")


STENCIL_TAPS = (
    (1, 0, 0, 0, 1.0),
    (-1, 0, 0, 0, 1.0),
    (0, 1, 0, 1, 1.0),
    (0, -1, 0, 1, 1.0),
    (0, 0, 1, 2, 1.0),
    (0, 0, -1, 2, 1.0),
    (1, 1, 0, 3, 0.5),
    (-1, -1, 0, 3, 0.5),
    (1, -1, 0, 3, -0.5),
    (-1, 1, 0, 3, -0.5),
    (1, 0, 1, 4, 0.5),
    (-1, 0, -1, 4, 0.5),
    (1, 0, -1, 4, -0.5),
    (-1, 0, 1, 4, -0.5),
    (0, 1, 1, 5, 0.5),
    (0, -1, -1, 5, 0.5),
    (0, 1, -1, 5, -0.5),
    (0, -1, 1, 5, -0.5),
)


def padded_2(cells, sides, width):
    for axis, dim in sides:
        count = lax.axis_size(axis)
        ends = count - 1
        head = lax.slice_in_dim(cells, 0, width, axis=dim)
        tail = lax.slice_in_dim(cells, cells.shape[dim] - width, cells.shape[dim], axis=dim)
        cells = jnp.concatenate(
            [
                lax.ppermute(tail, axis, [(i, (i + 1) % count) for i in range(ends)]),
                cells,
                lax.ppermute(head, axis, [((i + 1) % count, i) for i in range(ends)]),
            ],
            axis=dim,
        )
    return cells


def over_axes(shard, axes):
    return functools.reduce(lax.psum, axes, shard)


def shifted(padded, step_x, step_y, step_z):
    width_x = padded.shape[-3] - 2
    width_y = padded.shape[-2] - 2
    width_z = padded.shape[-1] - 2
    return padded[
        1 + step_x : 1 + step_x + width_x,
        1 + step_y : 1 + step_y + width_y,
        1 + step_z : 1 + step_z + width_z,
    ]


def edge_weights(tensors, step_x, step_y, step_z, component, factor):
    layer = tensors[component]
    return 0.5 * factor * (shifted(layer, 0, 0, 0) + shifted(layer, step_x, step_y, step_z))


def operate(padded, tensors):
    centre = shifted(padded, 0, 0, 0)
    accumulated = jnp.zeros_like(centre)
    for step_x, step_y, step_z, component, factor in STENCIL_TAPS:
        weight = edge_weights(tensors, step_x, step_y, step_z, component, factor)
        accumulated = accumulated + weight * (centre - shifted(padded, step_x, step_y, step_z))
    return accumulated


def class_onehot(labels, count):
    return (labels[..., None] == jnp.arange(count, dtype=jnp.int32)).astype(jnp.float32)


def reach_onehot(length, offset):
    position = jnp.arange(length, dtype=jnp.int32)
    relative = (position + offset) // length + 1
    return (relative[:, None] == jnp.arange(3, dtype=jnp.int32)[None, :]).astype(jnp.float32)


def reach_blocks(length, offset, blocks):
    block_span = length // blocks
    position = jnp.arange(length, dtype=jnp.int32)
    owning = (position // block_span)[:, None] == jnp.arange(blocks, dtype=jnp.int32)[None, :]
    relative = ((position % block_span + offset) // block_span + 1)[:, None] == jnp.arange(
        3, dtype=jnp.int32
    )[None, :]
    return (owning[:, :, None] & relative[:, None, :]).astype(jnp.float32)


def centre_mask():
    places = jnp.arange(3, dtype=jnp.int32)
    return (
        (places[:, None, None] == 1) & (places[None, :, None] == 1) & (places[None, None, :] == 1)
    )


def build_tensors(matches, scale, class_tensor):
    return (
        jnp.stack(
            [
                jnp.sum(
                    jnp.where(matches, class_tensor[component][:, None, None, None], 0.0), axis=0
                )
                for component in range(6)
            ]
        )
        * scale[None]
    )


def body(right_side, fiber_class, conductivity_scale, class_tensor, block_ids):
    highest = lax.Precision.HIGHEST
    kinds = jnp.arange(NCLS, dtype=jnp.int32)
    matches = fiber_class[None] == kinds[:, None, None, None]
    local_tensor = build_tensors(matches, conductivity_scale, class_tensor)
    tensors = padded_2(local_tensor, (("gx", 1), ("gy", 2), (GZ, 3)), 1)
    place_x = lax.axis_index("gx")
    place_y = lax.axis_index("gy")
    place_z = lax.axis_index(GZ)
    padded_ids = jnp.pad(block_ids, 1, constant_values=-1)
    window = lax.dynamic_slice(padded_ids, (place_x, place_y, place_z * ZBLK), (3, 3, ZBLK + 2))
    own_hot = class_onehot(window[1, 1, 1 : ZBLK + 1], COARSE)
    neighbours = jnp.stack([window[:, :, z_block : z_block + 3] for z_block in range(ZBLK)])
    rim_weight = jnp.zeros((ZBLK, 3, 3, 3), jnp.float32)
    for step_x, step_y, step_z, component, factor in STENCIL_TAPS:
        weight = edge_weights(tensors, step_x, step_y, step_z, component, factor)
        rim_weight = rim_weight + jnp.einsum(
            "xyz,xa,yb,zjc->jabc",
            weight,
            reach_onehot(CX, step_x),
            reach_onehot(CY, step_y),
            reach_blocks(CZ, step_z, ZBLK),
            precision=highest,
        )
    rim_weight = jnp.where(centre_mask()[None], 0.0, rim_weight)
    diagonal_terms = jnp.einsum(
        "jk,j->k", own_hot, jnp.sum(rim_weight, axis=(1, 2, 3)), precision=highest
    )
    coupling = jnp.einsum(
        "jk,jabc,jabcl->kl",
        own_hot,
        rim_weight,
        class_onehot(neighbours, COARSE),
        precision=highest,
    )
    coarse = over_axes(jnp.diag(diagonal_terms) - coupling, GX_GY_GZ)
    coarse = 0.5 * (coarse + coarse.T)
    factor_lower = jnp.linalg.cholesky(coarse)

    def restrict(field):
        block_totals = jnp.sum(field.reshape(CX, CY, ZBLK, BZ), axis=(0, 1, 3))
        return jnp.einsum("jk,j->k", own_hot, block_totals, precision=highest)

    def prolong(coarse_values):
        values = jnp.einsum("jk,k->j", own_hot, coarse_values, precision=highest)
        return jnp.broadcast_to(values[None, None, :, None], (CX, CY, ZBLK, BZ)).reshape(CX, CY, CZ)

    def apply_field(field):
        padded = padded_2(field, (("gx", 0), ("gy", 1), (GZ, 2)), 1)
        return operate(padded, tensors)

    def coarse_solve(field):
        projected = over_axes(restrict(field), GX_GY_GZ)
        return jax.scipy.linalg.cho_solve((factor_lower, True), projected)

    def deflation_image(coarse_values):
        beside_all = jnp.einsum(
            "abzk,k->abz", class_onehot(window, COARSE), coarse_values, precision=highest
        )
        beside_all = jnp.concatenate(
            [
                beside_all[0:1],
                jnp.broadcast_to(beside_all[1:2], (CX, 3, ZBLK + 2)),
                beside_all[2:3],
            ],
            axis=0,
        )
        beside_all = jnp.concatenate(
            [
                beside_all[:, 0:1],
                jnp.broadcast_to(beside_all[:, 1:2], (CX + 2, CY, ZBLK + 2)),
                beside_all[:, 2:3],
            ],
            axis=1,
        )
        beside_all = jnp.concatenate(
            [
                beside_all[:, :, 0:1],
                jnp.repeat(beside_all[:, :, 1 : ZBLK + 1], BZ, axis=2),
                beside_all[:, :, ZBLK + 1 :],
            ],
            axis=2,
        )
        result = operate(beside_all, tensors)
        return result

    coarse_values = coarse_solve(right_side)
    coarse_part = prolong(coarse_values)
    residual = right_side - deflation_image(coarse_values)
    estimate = jnp.zeros_like(right_side)

    def joint_terms(field):
        product = apply_field(field)
        projected, norm_value, cross_value = (
            over_axes(restrict(product), GX_GY_GZ),
            over_axes(jnp.sum(field * field), GX_GY_GZ),
            over_axes(jnp.sum(field * product), GX_GY_GZ),
        )
        correction = jax.scipy.linalg.cho_solve((factor_lower, True), projected)
        image_field = product - deflation_image(correction)
        return (image_field, norm_value, cross_value - jnp.sum(projected * correction))

    image_field, norm_now, curvature_now = joint_terms(residual)
    step_size = norm_now / curvature_now
    direction = residual
    along = image_field
    for iteration in range(ITERS):
        estimate = estimate + step_size * direction
        residual = residual - step_size * along
        if iteration + 1 < ITERS:
            image_field, norm_next, curvature_now = joint_terms(residual)
            step_ratio = norm_next / norm_now
            step_size = norm_next / (curvature_now - step_ratio * norm_next / step_size)
            direction = residual + step_ratio * direction
            along = image_field + step_ratio * along
            norm_now = norm_next
    solution = coarse_part + estimate - prolong(coarse_solve(apply_field(estimate)))
    return (solution, residual)


def solution(mesh):
    torus = Mesh(
        mesh.devices.reshape(mesh.shape["gx"], mesh.shape["gy"], 8, 2), ("gx", "gy", "gz_0", "gz_1")
    )
    return jax.shard_map(
        body,
        mesh=torus,
        in_specs=(P("gx", "gy", GZ), P("gx", "gy", GZ), P("gx", "gy", GZ), P(), P()),
        out_specs=(P("gx", "gy", GZ), P("gx", "gy", GZ)),
        check_vma=False,
    )
```

profile of v0, /device:TPU:1, one launch (start us, length us, event | category | flops | bytes accessed | tf_op | source)
XLA Modules:
  0.0 371.5 jit_solution(8955827215507283959)
XLA Ops:
  1.6 1.7 select_reduce_fusion
  4.2 4.8 %collective-permute-start = (f32[6,1,16,128]{3,2,1,0:T(8,128)S(1)}, f32[6,1,16,128]{3,2,1,0:T(8,128)S(1)}, u32[]{:S(2)}, u32[]{:S(2)}) collective-permute-start(f32[6,1,16,128]{3,2,1,0:T(8,128)S(1)} %get-tuple-element.65), channel_id=1, source_target_pairs={{0,64},{64,128},{128,192},{192,256},{256,320},{320,384},{384,448},... | collective-permute-start | bytes 147464 | tf_op jit(solution)/shard_map/ppermute | solution.py:51
  9.0 1.3 collective-permute-start.1
  11.4 3.1 collective-permute-done.1
  14.6 3.1 collective-permute-start.2
  17.7 1.3 collective-permute-start.3
  19.0 3.3 collective-permute-done.3
  23.1 6.3 %collective-permute-start.4 = (f32[6,10,18,1]{2,3,1,0:T(1,128)S(1)}, f32[6,10,18,1]{2,3,1,0:T(1,128)S(1)}, u32[]{:S(2)}, u32[]{:S(2)}) collective-permute-start(f32[6,10,18,1]{2,3,1,0:T(1,128)S(1)} %copy.197), channel_id=1, source_target_pairs={{0,1},{1,2},{2,3},{3,4},{4,5},{5,6},{6,7},{7,8},{8,9},{9,10},{10,1... | collective-permute-start | bytes 12968 | tf_op jit(solution)/shard_map/ppermute | solution.py:51
  30.0 1.9 collective-permute-start.5
  32.4 2.8 collective-permute-done.5
  46.7 26.4 %all-reduce.6 = (f32[64,64]{1,0:T(8,128)S(1)}, f32[64]{0:T(128)S(1)}) all-reduce(f32[64,64]{1,0:T(8,128)S(1)} %convolution_subtract_fusion, f32[64]{0:T(128)S(1)} %convolution_bitcast_fusion.24), channel_id=1, replica_groups=mesh['gx'=8,'gy'=4,'gz_0'=8,'gz_1'=2] {'gx'}, use_global_device_ids=true, to_apply=%region_7.8 | all-reduce | flops 4160 | bytes 33280 | tf_op jit(solution)/shard_map/psum | solution.py:61
  73.2 12.3 %all-reduce.9 = (f32[64,64]{1,0:T(8,128)S(1)}, f32[64]{0:T(128)S(1)}) all-reduce(f32[64,64]{1,0:T(8,128)S(1)} %get-tuple-element.33, f32[64]{0:T(128)S(1)} %get-tuple-element.34), channel_id=1, replica_groups=mesh['gx'=8,'gy'=4,'gz_0'=8,'gz_1'=2] {'gy'}, use_global_device_ids=true, to_apply=%region_8.9 | all-reduce | flops 4160 | bytes 33280 | tf_op jit(solution)/shard_map/psum | solution.py:61
  85.5 25.1 %all-reduce.3 = (f32[64,64]{1,0:T(8,128)S(1)}, f32[64]{0:T(128)S(1)}) all-reduce(f32[64,64]{1,0:T(8,128)S(1)} %get-tuple-element.41, f32[64]{0:T(128)S(1)} %get-tuple-element.42), channel_id=1, replica_groups=mesh['gx'=8,'gy'=4,'gz_0'=8,'gz_1'=2] {'gz_0'}, use_global_device_ids=true, to_apply=%region_9.10 | all-reduce | flops 4160 | bytes 33280 | tf_op jit(solution)/shard_map/psum | solution.py:61
  110.5 18.4 %all-reduce.12 = (f32[64,64]{1,0:T(8,128)S(1)}, f32[64]{0:T(128)S(1)}) all-reduce(f32[64,64]{1,0:T(8,128)S(1)} %get-tuple-element.25, f32[64]{0:T(128)S(1)} %get-tuple-element.26), channel_id=1, replica_groups=mesh['gx'=8,'gy'=4,'gz_0'=8,'gz_1'=2] {'gz_1'}, use_global_device_ids=true, to_apply=%region_10.11 | all-reduce | flops 4160 | bytes 33280 | tf_op jit(solution)/shard_map/psum | solution.py:61
  129.1 5.8 %cholesky.19 = f32[64,64]{1,0:T(8,128)S(1)} custom-call(f32[64,64]{1,0:T(8,128)S(1)} %fusion.311), custom_call_target="Cholesky" | custom-call | tf_op jit(solution)/shard_map/jit(cholesky)/cholesky | solution.py:167
  136.3 4.9 %custom-call.11 = f32[1,64,64]{1,2,0:T(8,128)S(1)} custom-call(f32[1,64,64]{2,1,0:T(8,128)S(1)} %fusion.299), custom_call_target="InvertDiagBlocksLowerTriangular" | custom-call | tf_op jit(solution)/shard_map/jit(_cho_solve)/triangular_solve | solution.py:183
  144.1 1.3 collective-permute-start.6
  145.4 4.0 %collective-permute-start.7 = (f32[1,16,128]{2,1,0:T(8,128)S(1)}, f32[1,16,128]{2,1,0:T(8,128)S(1)}, u32[]{:S(2)}, u32[]{:S(2)}) collective-permute-start(f32[1,16,128]{2,1,0:T(8,128)S(1)} %get-tuple-element.119), channel_id=1, source_target_pairs={{0,64},{64,128},{128,192},{192,256},{256,320},{320,384},{384,448},... | collective-permute-start | bytes 24584 | tf_op jit(solution)/shard_map/ppermute | solution.py:51
  150.2 1.3 collective-permute-start.8
  151.5 4.0 %collective-permute-start.9 = (f32[10,1,128]{2,1,0:T(1,128)S(1)}, f32[10,1,128]{2,1,0:T(1,128)S(1)}, u32[]{:S(2)}, u32[]{:S(2)}) collective-permute-start(f32[10,1,128]{2,1,0:T(1,128)S(1)} %get-tuple-element.113), channel_id=1, source_target_pairs={{0,16},{16,32},{32,48},{1,17},{17,33},{33,49},{2,18},{18,34},{34,5... | collective-permute-start | bytes 15368 | tf_op jit(solution)/shard_map/ppermute | solution.py:51
  156.4 4.3 %collective-permute-start.10 = (f32[10,18,1]{2,1,0:T(8,128)S(1)}, f32[10,18,1]{2,1,0:T(8,128)S(1)}, u32[]{:S(2)}, u32[]{:S(2)}) collective-permute-start(f32[10,18,1]{2,1,0:T(8,128)S(1)} %get-tuple-element.90), channel_id=1, source_target_pairs={{1,0},{2,1},{3,2},{4,3},{5,4},{6,5},{7,6},{8,7},{9,8},{10,9},{11,1... | collective-permute-start | bytes 2168 | tf_op jit(solution)/shard_map/ppermute | solution.py:53
  160.7 2.5 collective-permute-start.11
  163.7 1.2 collective-permute-done.11
  166.4 14.5 %all-reduce.5 = (f32[64]{0:T(128)S(1)}, f32[]{:T(128)}, f32[]{:T(128)}) all-reduce(f32[64]{0:T(128)S(1)} %convolution_bitcast_fusion.22, f32[]{:T(128)} %get-tuple-element.12, f32[]{:T(128)} %get-tuple-element.10), channel_id=1, replica_groups=mesh['gx'=8,'gy'=4,'gz_0'=8,'gz_1'=2] {'gx'}, use_global_device_ids=true, to_apply=%region_31.33 | all-reduce | flops 66 | bytes 528 | tf_op jit(solution)/shard_map/psum | solution.py:61
  180.9 8.6 %all-reduce.8 = (f32[64]{0:T(128)S(1)}, f32[]{:T(128)}, f32[]{:T(128)}) all-reduce(f32[64]{0:T(128)S(1)} %get-tuple-element.30, f32[]{:T(128)} %get-tuple-element.31, f32[]{:T(128)} %get-tuple-element.32), channel_id=1, replica_groups=mesh['gx'=8,'gy'=4,'gz_0'=8,'gz_1'=2] {'gy'}, use_global_device_ids=true, to_apply=%region_32.34 | all-reduce | flops 66 | bytes 528 | tf_op jit(solution)/shard_map/psum | solution.py:61
  189.5 12.7 %all-reduce.2 = (f32[64]{0:T(128)S(1)}, f32[]{:T(128)}, f32[]{:T(128)}) all-reduce(f32[64]{0:T(128)S(1)} %get-tuple-element.38, f32[]{:T(128)} %get-tuple-element.39, f32[]{:T(128)} %get-tuple-element.40), channel_id=1, replica_groups=mesh['gx'=8,'gy'=4,'gz_0'=8,'gz_1'=2] {'gz_0'}, use_global_device_ids=true, to_apply=%region_33.35 | all-reduce | flops 66 | bytes 528 | tf_op jit(solution)/shard_map/psum | solution.py:61
  202.2 14.6 %all-reduce.11 = (f32[64]{0:T(128)S(1)}, f32[]{:T(128)}, f32[]{:T(128)}) all-reduce(f32[64]{0:T(128)S(1)} %get-tuple-element.22, f32[]{:T(128)} %get-tuple-element.23, f32[]{:T(128)} %get-tuple-element.24), channel_id=1, replica_groups=mesh['gx'=8,'gy'=4,'gz_0'=8,'gz_1'=2] {'gz_1'}, use_global_device_ids=true, to_apply=%region_34.36 | all-reduce | flops 66 | bytes 528 | tf_op jit(solution)/shard_map/psum | solution.py:61
  222.4 1.3 collective-permute-start.12
  223.7 4.0 %collective-permute-start.13 = (f32[1,16,128]{2,1,0:T(8,128)S(1)}, f32[1,16,128]{2,1,0:T(8,128)S(1)}, u32[]{:S(2)}, u32[]{:S(2)}) collective-permute-start(f32[1,16,128]{2,1,0:T(8,128)S(1)} %get-tuple-element.117), channel_id=1, source_target_pairs={{0,64},{64,128},{128,192},{192,256},{256,320},{320,384},{384,448},... | collective-permute-start | bytes 24584 | tf_op jit(solution)/shard_map/ppermute | solution.py:51
  228.5 1.3 collective-permute-start.14
  229.8 4.0 %collective-permute-start.15 = (f32[10,1,128]{2,1,0:T(1,128)S(1)}, f32[10,1,128]{2,1,0:T(1,128)S(1)}, u32[]{:S(2)}, u32[]{:S(2)}) collective-permute-start(f32[10,1,128]{2,1,0:T(1,128)S(1)} %get-tuple-element.109), channel_id=1, source_target_pairs={{0,16},{16,32},{32,48},{1,17},{17,33},{33,49},{2,18},{18,34},{34,5... | collective-permute-start | bytes 15368 | tf_op jit(solution)/shard_map/ppermute | solution.py:51
  234.7 4.5 %collective-permute-start.16 = (f32[10,18,1]{2,1,0:T(8,128)S(1)}, f32[10,18,1]{2,1,0:T(8,128)S(1)}, u32[]{:S(2)}, u32[]{:S(2)}) collective-permute-start(f32[10,18,1]{2,1,0:T(8,128)S(1)} %get-tuple-element.88), channel_id=1, source_target_pairs={{1,0},{2,1},{3,2},{4,3},{5,4},{6,5},{7,6},{8,7},{9,8},{10,9},{11,1... | collective-permute-start | bytes 2168 | tf_op jit(solution)/shard_map/ppermute | solution.py:53
  239.2 1.9 collective-permute-start.17
  241.5 1.4 collective-permute-done.17
  244.4 13.9 %all-reduce.4 = (f32[]{:T(128)}, f32[]{:T(128)}, f32[64]{0:T(128)S(1)}) all-reduce(f32[]{:T(128)} %get-tuple-element.9, f32[]{:T(128)} %get-tuple-element.8, f32[64]{0:T(128)S(1)} %convolution_bitcast_fusion.21), channel_id=1, replica_groups=mesh['gx'=8,'gy'=4,'gz_0'=8,'gz_1'=2] {'gx'}, use_global_device_ids=true, to_apply=%region_37.39 | all-reduce | flops 66 | bytes 528 | tf_op jit(solution)/shard_map/psum | solution.py:61
  258.3 8.6 %all-reduce.7 = (f32[]{:T(128)}, f32[]{:T(128)}, f32[64]{0:T(128)S(1)}) all-reduce(f32[]{:T(128)} %get-tuple-element.27, f32[]{:T(128)} %get-tuple-element.28, f32[64]{0:T(128)S(1)} %get-tuple-element.29), channel_id=1, replica_groups=mesh['gx'=8,'gy'=4,'gz_0'=8,'gz_1'=2] {'gy'}, use_global_device_ids=true, to_apply=%region_38.40 | all-reduce | flops 66 | bytes 528 | tf_op jit(solution)/shard_map/psum | solution.py:61
  266.9 12.5 %all-reduce.1 = (f32[]{:T(128)}, f32[]{:T(128)}, f32[64]{0:T(128)S(1)}) all-reduce(f32[]{:T(128)} %get-tuple-element.35, f32[]{:T(128)} %get-tuple-element.36, f32[64]{0:T(128)S(1)} %get-tuple-element.37), channel_id=1, replica_groups=mesh['gx'=8,'gy'=4,'gz_0'=8,'gz_1'=2] {'gz_0'}, use_global_device_ids=true, to_apply=%region_39.41 | all-reduce | flops 66 | bytes 528 | tf_op jit(solution)/shard_map/psum | solution.py:61
  279.4 14.5 %all-reduce.10 = (f32[]{:T(128)}, f32[]{:T(128)}, f32[64]{0:T(128)S(1)}) all-reduce(f32[]{:T(128)} %get-tuple-element.19, f32[]{:T(128)} %get-tuple-element.20, f32[64]{0:T(128)S(1)} %get-tuple-element.21), channel_id=1, replica_groups=mesh['gx'=8,'gy'=4,'gz_0'=8,'gz_1'=2] {'gz_1'}, use_global_device_ids=true, to_apply=%region_40.42 | all-reduce | flops 66 | bytes 528 | tf_op jit(solution)/shard_map/psum | solution.py:61
  300.6 1.3 collective-permute-start.18
  301.9 4.0 %collective-permute-start.19 = (f32[1,16,128]{2,1,0:T(8,128)S(1)}, f32[1,16,128]{2,1,0:T(8,128)S(1)}, u32[]{:S(2)}, u32[]{:S(2)}) collective-permute-start(f32[1,16,128]{2,1,0:T(8,128)S(1)} %get-tuple-element.115), channel_id=1, source_target_pairs={{0,64},{64,128},{128,192},{192,256},{256,320},{320,384},{384,448},... | collective-permute-start | bytes 24584 | tf_op jit(solution)/shard_map/ppermute | solution.py:51
  307.1 1.3 collective-permute-start.20
  308.4 4.0 %collective-permute-start.21 = (f32[10,1,128]{2,1,0:T(1,128)S(1)}, f32[10,1,128]{2,1,0:T(1,128)S(1)}, u32[]{:S(2)}, u32[]{:S(2)}) collective-permute-start(f32[10,1,128]{2,1,0:T(1,128)S(1)} %get-tuple-element.105), channel_id=1, source_target_pairs={{0,16},{16,32},{32,48},{1,17},{17,33},{33,49},{2,18},{18,34},{34,5... | collective-permute-start | bytes 15368 | tf_op jit(solution)/shard_map/ppermute | solution.py:51
  313.5 3.9 %collective-permute-start.22 = (f32[10,18,1]{2,1,0:T(8,128)S(1)}, f32[10,18,1]{2,1,0:T(8,128)S(1)}, u32[]{:S(2)}, u32[]{:S(2)}) collective-permute-start(f32[10,18,1]{2,1,0:T(8,128)S(1)} %get-tuple-element.86), channel_id=1, source_target_pairs={{1,0},{2,1},{3,2},{4,3},{5,4},{6,5},{7,6},{8,7},{9,8},{10,9},{11,1... | collective-permute-start | bytes 2168 | tf_op jit(solution)/shard_map/ppermute | solution.py:53
  317.4 2.2 collective-permute-start.23
  322.3 14.0 %psum.284 = f32[64]{0:T(128)S(1)} all-reduce(f32[64]{0:T(128)S(1)} %convolution_bitcast_fusion.20), channel_id=1, replica_groups=mesh['gx'=8,'gy'=4,'gz_0'=8,'gz_1'=2] {'gx'}, use_global_device_ids=true, to_apply=%region_55.57 | all-reduce | flops 64 | bytes 512 | tf_op jit(solution)/shard_map/psum | solution.py:61
  336.2 8.0 %psum.285 = f32[64]{0:T(128)S(1)} all-reduce(f32[64]{0:T(128)S(1)} %psum.284), channel_id=1, replica_groups=mesh['gx'=8,'gy'=4,'gz_0'=8,'gz_1'=2] {'gy'}, use_global_device_ids=true, to_apply=%region_56.58 | all-reduce | flops 64 | bytes 512 | tf_op jit(solution)/shard_map/psum | solution.py:61
  344.2 12.2 %psum.286 = f32[64]{0:T(128)S(1)} all-reduce(f32[64]{0:T(128)S(1)} %psum.285), channel_id=1, replica_groups=mesh['gx'=8,'gy'=4,'gz_0'=8,'gz_1'=2] {'gz_0'}, use_global_device_ids=true, to_apply=%region_57.59 | all-reduce | flops 64 | bytes 512 | tf_op jit(solution)/shard_map/psum | solution.py:61
  356.4 13.7 %psum.287 = f32[64]{0:T(128)S(1)} all-reduce(f32[64]{0:T(128)S(1)} %psum.286), channel_id=1, replica_groups=mesh['gx'=8,'gy'=4,'gz_0'=8,'gz_1'=2] {'gz_1'}, use_global_device_ids=true, to_apply=%region_58.60 | all-reduce | flops 64 | bytes 512 | tf_op jit(solution)/shard_map/psum | solution.py:61
  (233 shorter events, 39.1 us)
Async XLA Ops:
  0.6 10.0 %copy-start.1 = (s32[8,4,32]{2,1,0:T(4,128)S(1)}, s32[8,4,32]{2,1,0:T(4,128)}, u32[]{:S(2)}) copy-start(s32[8,4,32]{2,1,0:T(4,128)} %param.11) | copy-start | bytes 12292
  0.6 10.2 %copy-start = (f32[8,16,128]{2,1,0:T(8,128)S(1)}, f32[8,16,128]{2,1,0:T(8,128)}, u32[]{:S(2)}) copy-start(f32[8,16,128]{2,1,0:T(8,128)} %param.7) | copy-start | bytes 196612
  4.2 7.2 %collective-permute-start = (f32[6,1,16,128]{3,2,1,0:T(8,128)S(1)}, f32[6,1,16,128]{3,2,1,0:T(8,128)S(1)}, u32[]{:S(2)}, u32[]{:S(2)}) collective-permute-start(f32[6,1,16,128]{3,2,1,0:T(8,128)S(1)} %get-tuple-element.65), channel_id=1, source_target_pairs={{0,64},{64,128},{128,192},{192,256},{256,320},{320,384},{384,448},... | collective-permute-start | bytes 147464 | tf_op jit(solution)/shard_map/ppermute | solution.py:51
  9.0 5.5 %collective-permute-start.1 = (f32[6,1,16,128]{3,2,1,0:T(8,128)S(1)}, f32[6,1,16,128]{3,2,1,0:T(8,128)S(1)}, u32[]{:S(2)}, u32[]{:S(2)}) collective-permute-start(f32[6,1,16,128]{3,2,1,0:T(8,128)S(1)} %get-tuple-element.66), channel_id=1, source_target_pairs={{64,0},{128,64},{192,128},{256,192},{320,256},{384,320},{448,384},... | collective-permute-start | bytes 147464 | tf_op jit(solution)/shard_map/ppermute | solution.py:53
  14.6 4.4 %collective-permute-start.2 = (f32[6,10,1,128]{3,2,1,0:T(1,128)S(1)}, f32[6,10,1,128]{3,2,1,0:T(1,128)S(1)}, u32[]{:S(2)}, u32[]{:S(2)}) collective-permute-start(f32[6,10,1,128]{3,2,1,0:T(1,128)S(1)} %get-tuple-element.63), channel_id=1, source_target_pairs={{0,16},{16,32},{32,48},{1,17},{17,33},{33,49},{2,18},{18,34},{34,5... | collective-permute-start | bytes 92168 | tf_op jit(solution)/shard_map/ppermute | solution.py:51
  17.7 4.6 %collective-permute-start.3 = (f32[6,10,1,128]{3,2,1,0:T(1,128)S(1)}, f32[6,10,1,128]{3,2,1,0:T(1,128)S(1)}, u32[]{:S(2)}, u32[]{:S(2)}) collective-permute-start(f32[6,10,1,128]{3,2,1,0:T(1,128)S(1)} %get-tuple-element.64), channel_id=1, source_target_pairs={{16,0},{32,16},{48,32},{17,1},{33,17},{49,33},{18,2},{34,18},{50,3... | collective-permute-start | bytes 92168 | tf_op jit(solution)/shard_map/ppermute | solution.py:53
  23.1 8.7 %collective-permute-start.4 = (f32[6,10,18,1]{2,3,1,0:T(1,128)S(1)}, f32[6,10,18,1]{2,3,1,0:T(1,128)S(1)}, u32[]{:S(2)}, u32[]{:S(2)}) collective-permute-start(f32[6,10,18,1]{2,3,1,0:T(1,128)S(1)} %copy.197), channel_id=1, source_target_pairs={{0,1},{1,2},{2,3},{3,4},{4,5},{5,6},{6,7},{7,8},{8,9},{9,10},{10,1... | collective-permute-start | bytes 12968 | tf_op jit(solution)/shard_map/ppermute | solution.py:51
  30.0 5.2 %collective-permute-start.5 = (f32[6,10,18,1]{2,3,1,0:T(1,128)S(1)}, f32[6,10,18,1]{2,3,1,0:T(1,128)S(1)}, u32[]{:S(2)}, u32[]{:S(2)}) collective-permute-start(f32[6,10,18,1]{2,3,1,0:T(1,128)S(1)} %copy.198), channel_id=1, source_target_pairs={{1,0},{2,1},{3,2},{4,3},{5,4},{6,5},{7,6},{8,7},{9,8},{10,9},{11,1... | collective-permute-start | bytes 12968 | tf_op jit(solution)/shard_map/ppermute | solution.py:53
  144.1 5.3 %collective-permute-start.6 = (f32[1,16,128]{2,1,0:T(8,128)S(1)}, f32[1,16,128]{2,1,0:T(8,128)S(1)}, u32[]{:S(2)}, u32[]{:S(2)}) collective-permute-start(f32[1,16,128]{2,1,0:T(8,128)S(1)} %get-tuple-element.120), channel_id=1, source_target_pairs={{64,0},{128,64},{192,128},{256,192},{320,256},{384,320},{448,384},... | collective-permute-start | bytes 24584 | tf_op jit(solution)/shard_map/ppermute | solution.py:53
  145.4 4.8 %collective-permute-start.7 = (f32[1,16,128]{2,1,0:T(8,128)S(1)}, f32[1,16,128]{2,1,0:T(8,128)S(1)}, u32[]{:S(2)}, u32[]{:S(2)}) collective-permute-start(f32[1,16,128]{2,1,0:T(8,128)S(1)} %get-tuple-element.119), channel_id=1, source_target_pairs={{0,64},{64,128},{128,192},{192,256},{256,320},{320,384},{384,448},... | collective-permute-start | bytes 24584 | tf_op jit(solution)/shard_map/ppermute | solution.py:51
  150.2 5.3 %collective-permute-start.8 = (f32[10,1,128]{2,1,0:T(1,128)S(1)}, f32[10,1,128]{2,1,0:T(1,128)S(1)}, u32[]{:S(2)}, u32[]{:S(2)}) collective-permute-start(f32[10,1,128]{2,1,0:T(1,128)S(1)} %get-tuple-element.114), channel_id=1, source_target_pairs={{16,0},{32,16},{48,32},{17,1},{33,17},{49,33},{18,2},{34,18},{50,3... | collective-permute-start | bytes 15368 | tf_op jit(solution)/shard_map/ppermute | solution.py:53
  151.5 4.7 %collective-permute-start.9 = (f32[10,1,128]{2,1,0:T(1,128)S(1)}, f32[10,1,128]{2,1,0:T(1,128)S(1)}, u32[]{:S(2)}, u32[]{:S(2)}) collective-permute-start(f32[10,1,128]{2,1,0:T(1,128)S(1)} %get-tuple-element.113), channel_id=1, source_target_pairs={{0,16},{16,32},{32,48},{1,17},{17,33},{33,49},{2,18},{18,34},{34,5... | collective-permute-start | bytes 15368 | tf_op jit(solution)/shard_map/ppermute | solution.py:51
  156.4 7.3 %collective-permute-start.10 = (f32[10,18,1]{2,1,0:T(8,128)S(1)}, f32[10,18,1]{2,1,0:T(8,128)S(1)}, u32[]{:S(2)}, u32[]{:S(2)}) collective-permute-start(f32[10,18,1]{2,1,0:T(8,128)S(1)} %get-tuple-element.90), channel_id=1, source_target_pairs={{1,0},{2,1},{3,2},{4,3},{5,4},{6,5},{7,6},{8,7},{9,8},{10,9},{11,1... | collective-permute-start | bytes 2168 | tf_op jit(solution)/shard_map/ppermute | solution.py:53
  160.7 4.2 %collective-permute-start.11 = (f32[10,18,1]{2,1,0:T(8,128)S(1)}, f32[10,18,1]{2,1,0:T(8,128)S(1)}, u32[]{:S(2)}, u32[]{:S(2)}) collective-permute-start(f32[10,18,1]{2,1,0:T(8,128)S(1)} %get-tuple-element.89), channel_id=1, source_target_pairs={{0,1},{1,2},{2,3},{3,4},{4,5},{5,6},{6,7},{7,8},{8,9},{9,10},{10,1... | collective-permute-start | bytes 2168 | tf_op jit(solution)/shard_map/ppermute | solution.py:51
  222.4 5.3 %collective-permute-start.12 = (f32[1,16,128]{2,1,0:T(8,128)S(1)}, f32[1,16,128]{2,1,0:T(8,128)S(1)}, u32[]{:S(2)}, u32[]{:S(2)}) collective-permute-start(f32[1,16,128]{2,1,0:T(8,128)S(1)} %get-tuple-element.118), channel_id=1, source_target_pairs={{64,0},{128,64},{192,128},{256,192},{320,256},{384,320},{448,384},... | collective-permute-start | bytes 24584 | tf_op jit(solution)/shard_map/ppermute | solution.py:53
  223.7 4.8 %collective-permute-start.13 = (f32[1,16,128]{2,1,0:T(8,128)S(1)}, f32[1,16,128]{2,1,0:T(8,128)S(1)}, u32[]{:S(2)}, u32[]{:S(2)}) collective-permute-start(f32[1,16,128]{2,1,0:T(8,128)S(1)} %get-tuple-element.117), channel_id=1, source_target_pairs={{0,64},{64,128},{128,192},{192,256},{256,320},{320,384},{384,448},... | collective-permute-start | bytes 24584 | tf_op jit(solution)/shard_map/ppermute | solution.py:51
  228.5 5.6 %collective-permute-start.14 = (f32[10,1,128]{2,1,0:T(1,128)S(1)}, f32[10,1,128]{2,1,0:T(1,128)S(1)}, u32[]{:S(2)}, u32[]{:S(2)}) collective-permute-start(f32[10,1,128]{2,1,0:T(1,128)S(1)} %get-tuple-element.110), channel_id=1, source_target_pairs={{16,0},{32,16},{48,32},{17,1},{33,17},{49,33},{18,2},{34,18},{50,3... | collective-permute-start | bytes 15368 | tf_op jit(solution)/shard_map/ppermute | solution.py:53
  229.8 4.7 %collective-permute-start.15 = (f32[10,1,128]{2,1,0:T(1,128)S(1)}, f32[10,1,128]{2,1,0:T(1,128)S(1)}, u32[]{:S(2)}, u32[]{:S(2)}) collective-permute-start(f32[10,1,128]{2,1,0:T(1,128)S(1)} %get-tuple-element.109), channel_id=1, source_target_pairs={{0,16},{16,32},{32,48},{1,17},{17,33},{33,49},{2,18},{18,34},{34,5... | collective-permute-start | bytes 15368 | tf_op jit(solution)/shard_map/ppermute | solution.py:51
  234.7 6.9 %collective-permute-start.16 = (f32[10,18,1]{2,1,0:T(8,128)S(1)}, f32[10,18,1]{2,1,0:T(8,128)S(1)}, u32[]{:S(2)}, u32[]{:S(2)}) collective-permute-start(f32[10,18,1]{2,1,0:T(8,128)S(1)} %get-tuple-element.88), channel_id=1, source_target_pairs={{1,0},{2,1},{3,2},{4,3},{5,4},{6,5},{7,6},{8,7},{9,8},{10,9},{11,1... | collective-permute-start | bytes 2168 | tf_op jit(solution)/shard_map/ppermute | solution.py:53
  239.2 3.8 %collective-permute-start.17 = (f32[10,18,1]{2,1,0:T(8,128)S(1)}, f32[10,18,1]{2,1,0:T(8,128)S(1)}, u32[]{:S(2)}, u32[]{:S(2)}) collective-permute-start(f32[10,18,1]{2,1,0:T(8,128)S(1)} %get-tuple-element.87), channel_id=1, source_target_pairs={{0,1},{1,2},{2,3},{3,4},{4,5},{5,6},{6,7},{7,8},{8,9},{9,10},{10,1... | collective-permute-start | bytes 2168 | tf_op jit(solution)/shard_map/ppermute | solution.py:51
  300.6 6.4 %collective-permute-start.18 = (f32[1,16,128]{2,1,0:T(8,128)S(1)}, f32[1,16,128]{2,1,0:T(8,128)S(1)}, u32[]{:S(2)}, u32[]{:S(2)}) collective-permute-start(f32[1,16,128]{2,1,0:T(8,128)S(1)} %get-tuple-element.116), channel_id=1, source_target_pairs={{64,0},{128,64},{192,128},{256,192},{320,256},{384,320},{448,384},... | collective-permute-start | bytes 24584 | tf_op jit(solution)/shard_map/ppermute | solution.py:53
  301.9 5.1 %collective-permute-start.19 = (f32[1,16,128]{2,1,0:T(8,128)S(1)}, f32[1,16,128]{2,1,0:T(8,128)S(1)}, u32[]{:S(2)}, u32[]{:S(2)}) collective-permute-start(f32[1,16,128]{2,1,0:T(8,128)S(1)} %get-tuple-element.115), channel_id=1, source_target_pairs={{0,64},{64,128},{128,192},{192,256},{256,320},{320,384},{384,448},... | collective-permute-start | bytes 24584 | tf_op jit(solution)/shard_map/ppermute | solution.py:51
  307.1 6.3 %collective-permute-start.20 = (f32[10,1,128]{2,1,0:T(1,128)S(1)}, f32[10,1,128]{2,1,0:T(1,128)S(1)}, u32[]{:S(2)}, u32[]{:S(2)}) collective-permute-start(f32[10,1,128]{2,1,0:T(1,128)S(1)} %get-tuple-element.106), channel_id=1, source_target_pairs={{16,0},{32,16},{48,32},{17,1},{33,17},{49,33},{18,2},{34,18},{50,3... | collective-permute-start | bytes 15368 | tf_op jit(solution)/shard_map/ppermute | solution.py:53
  308.4 5.0 %collective-permute-start.21 = (f32[10,1,128]{2,1,0:T(1,128)S(1)}, f32[10,1,128]{2,1,0:T(1,128)S(1)}, u32[]{:S(2)}, u32[]{:S(2)}) collective-permute-start(f32[10,1,128]{2,1,0:T(1,128)S(1)} %get-tuple-element.105), channel_id=1, source_target_pairs={{0,16},{16,32},{32,48},{1,17},{17,33},{33,49},{2,18},{18,34},{34,5... | collective-permute-start | bytes 15368 | tf_op jit(solution)/shard_map/ppermute | solution.py:51
  313.5 6.7 %collective-permute-start.22 = (f32[10,18,1]{2,1,0:T(8,128)S(1)}, f32[10,18,1]{2,1,0:T(8,128)S(1)}, u32[]{:S(2)}, u32[]{:S(2)}) collective-permute-start(f32[10,18,1]{2,1,0:T(8,128)S(1)} %get-tuple-element.86), channel_id=1, source_target_pairs={{1,0},{2,1},{3,2},{4,3},{5,4},{6,5},{7,6},{8,7},{9,8},{10,9},{11,1... | collective-permute-start | bytes 2168 | tf_op jit(solution)/shard_map/ppermute | solution.py:53
  317.4 4.0 %collective-permute-start.23 = (f32[10,18,1]{2,1,0:T(8,128)S(1)}, f32[10,18,1]{2,1,0:T(8,128)S(1)}, u32[]{:S(2)}, u32[]{:S(2)}) collective-permute-start(f32[10,18,1]{2,1,0:T(8,128)S(1)} %get-tuple-element.85), channel_id=1, source_target_pairs={{0,1},{1,2},{2,3},{3,4},{4,5},{5,6},{6,7},{7,8},{8,9},{9,10},{10,1... | collective-permute-start | bytes 2168 | tf_op jit(solution)/shard_map/ppermute | solution.py:51
where the time goes:
time: 373 us; the launch traced here: 371 us
  blocking collectives  230 us (62%)
  starting transfers between devices  69.8 us (19%)
  other arithmetic  22.8 us (6%)
  waiting for transfers between devices  17.2 us (5%)
  matrix products  14.2 us (4%)
  local copies, waits for them, and re-layouts  9.17 us (2%)
  between operations  8.21 us (2%)
    psum x16, blocking collectives, over_axes(): return functools.reduce(lax.psum, axes, shard)  230 us
    ppermute x12, starting transfers between devices, padded_2(): lax.ppermute(tail, axis, [(i, (i + 1) % count) for i in range(ends)])  44.8 us
    ppermute x12, starting transfers between devices, padded_2(): lax.ppermute(head, axis, [((i + 1) % count, i) for i in range(ends)])  25 us
    ppermute x12, waiting for transfers between devices, padded_2(): lax.ppermute(head, axis, [((i + 1) % count, i) for i in range(ends)])  10.6 us
    dot_general x54, matrix products, body(): jnp.einsum('xyz,xa,yb,zjc->jabc', weight, reach_onehot(CX, step_x), reach...  8.59 us
  transfers between devices with their start and end apart: 24, of which 13 were waited for; matrix products, arithmetic and copies ran while one was open for 1% of the time, Pallas kernels for 0%

commit v1 on v0

v1 whole, which is shorter than its diff:
```python
import functools

import jax
import jax.numpy as jnp
import numpy as np
from jax import lax
from jax.experimental import pallas as pl
from jax.experimental.pallas import tpu as pltpu
from jax.sharding import PartitionSpec as P

COARSE = 64
NCLS = 16
ZBLK = 2
HALO = 3
LANES = 128
EY = 24
EZ = 256
SLOTS = 32
HIGHEST = lax.Precision.HIGHEST

STENCIL_TAPS = (
    (1, 0, 0, 0, 1.0),
    (-1, 0, 0, 0, 1.0),
    (0, 1, 0, 1, 1.0),
    (0, -1, 0, 1, 1.0),
    (0, 0, 1, 2, 1.0),
    (0, 0, -1, 2, 1.0),
    (1, 1, 0, 3, 0.5),
    (-1, -1, 0, 3, 0.5),
    (1, -1, 0, 3, -0.5),
    (-1, 1, 0, 3, -0.5),
    (1, 0, 1, 4, 0.5),
    (-1, 0, -1, 4, 0.5),
    (1, 0, -1, 4, -0.5),
    (-1, 0, 1, 4, -0.5),
    (0, 1, 1, 5, 0.5),
    (0, -1, -1, 5, 0.5),
    (0, 1, -1, 5, -0.5),
    (0, -1, 1, 5, -0.5),
)
EDGES = (
    (1, 0, 0, 0, 1.0),
    (0, 1, 0, 1, 1.0),
    (0, 0, 1, 2, 1.0),
    (1, 1, 0, 3, 0.5),
    (1, -1, 0, 3, -0.5),
    (1, 0, 1, 4, 0.5),
    (1, 0, -1, 4, -0.5),
    (0, 1, 1, 5, 0.5),
    (0, 1, -1, 5, -0.5),
)
NEIGHBOURS = tuple(
    (a, b, c)
    for a in (-1, 0, 1)
    for b in (-1, 0, 1)
    for c in (-1, 0, 1)
    if 1 <= abs(a) + abs(b) + abs(c) <= 2
)
NNB = len(NEIGHBOURS)
RHS_SLOT = NNB
ROWS = 56
VMEM = pl.BlockSpec(memory_space=pltpu.VMEM)
SMEM = pl.BlockSpec(memory_space=pltpu.SMEM)


def crossing_table():
    table = np.zeros((3, SLOTS, ROWS), np.float32)

    def cells(step, reach):
        if step == 0:
            return ((2, 1.0),) if reach == 0 else ()
        edge = 1 if step > 0 else 0
        if reach == step:
            return ((edge, 1.0),)
        return ((2, 1.0), (edge, -1.0)) if reach == 0 else ()

    for sx, sy, sz, component, factor in STENCIL_TAPS:
        for slot, (a, b, c) in enumerate(NEIGHBOURS):
            for px, fx in cells(sx, a):
                for py, fy in cells(sy, b):
                    for pz, fz in cells(sz, c):
                        table[pz, slot, component * 9 + px * 3 + py] += 0.5 * factor * fx * fy * fz
    table[2, RHS_SLOT, 54] = 1.0
    return table.reshape(3 * SLOTS, ROWS)


def lookup(kinds, scale, table):
    values = [jnp.full(scale.shape, table[c, 0], jnp.float32) for c in range(6)]
    for kind in range(1, NCLS):
        hit = kinds == kind
        values = [jnp.where(hit, table[c, kind], values[c]) for c in range(6)]
    return [value * scale for value in values]


def lane_ids(shape):
    return lax.broadcasted_iota(jnp.int32, shape, len(shape) - 1)


def row_ids(shape):
    return lax.broadcasted_iota(jnp.int32, shape, len(shape) - 2)


def own_sums_kernel(table_ref, source_ref, kinds_ref, scale_ref, crossing_ref, out_ref, rows_ref):
    cx, cy, cz = source_ref.shape
    rows_ref[...] = jnp.zeros_like(rows_ref)
    firsts, totals = None, None
    total_source = None
    for x in range(cx):
        layers = lookup(kinds_ref[x], scale_ref[x], table_ref)
        total_source = source_ref[x] if x == 0 else total_source + source_ref[x]
        if x == 0:
            firsts, totals = layers, layers
        else:
            totals = [t + v for t, v in zip(totals, layers)]
    for c in range(6):
        for px, field in enumerate((firsts[c], layers[c], totals[c])):
            at = c * 9 + px * 3
            rows_ref[at : at + 1, :] = field[0:1]
            rows_ref[at + 1 : at + 2, :] = field[cy - 1 : cy]
            rows_ref[at + 2 : at + 3, :] = jnp.sum(field, axis=0, keepdims=True)
    rows_ref[54:55, :] = jnp.sum(total_source, axis=0, keepdims=True)
    sums = jnp.dot(crossing_ref[...], rows_ref[...], precision=HIGHEST, preferred_element_type=jnp.float32)
    block = cz // ZBLK
    lane = lane_ids((SLOTS, cz))
    picked = (
        jnp.where(lane % block == 0, sums[:SLOTS], 0.0)
        + jnp.where(lane % block == block - 1, sums[SLOTS : 2 * SLOTS], 0.0)
        + sums[2 * SLOTS :]
    )
    spread = jnp.concatenate([picked] * ZBLK + [jnp.zeros((LANES - ZBLK * SLOTS, cz), jnp.float32)], axis=0)
    group = row_ids((LANES, cz)) // SLOTS
    spread = jnp.where(lane_ids((LANES, cz)) // block == group, spread, 0.0)
    row = lax.dot_general(
        jnp.ones((8, cz), jnp.float32), spread, (((1,), (1,)), ((), ())),
        precision=HIGHEST, preferred_element_type=jnp.float32,
    )
    out_ref[...] = jnp.broadcast_to(row[0:1].reshape(1, 1, LANES), out_ref.shape)


def shift_z(x, step):
    return pltpu.roll(x, (-step) % EZ, 1)


def shift_y(x, step):
    return pltpu.roll(x, (-step) % EY, 0)


def shift(x, step_y, step_z):
    if step_y:
        x = shift_y(x, step_y)
    if step_z:
        x = shift_z(x, step_z)
    return x


def weights_kernel(table_ref, kinds_ref, scale_ref, out_ref, layers_ref):
    planes = scale_ref.shape[0]

    def fill(p, carry):
        for c, layer in enumerate(lookup(kinds_ref[p], scale_ref[p], table_ref)):
            layers_ref[c, p] = layer
        return carry

    lax.fori_loop(0, planes, fill, 0)

    def edges(p, carry):
        after = jnp.minimum(p + 1, planes - 1)
        for e, (sx, sy, sz, c, factor) in enumerate(EDGES):
            beside = layers_ref[c, after] if sx else layers_ref[c, p]
            out_ref[e, p] = (0.5 * factor) * (layers_ref[c, p] + shift(beside, sy, sz))
        return carry

    lax.fori_loop(0, planes, edges, 0)


def across(here, after, weights, p):
    g1 = weights[0, p] * (here - after)
    g2 = weights[3, p] * (here - shift_y(after, 1))
    g3 = weights[4, p] * (here - shift_y(after, -1))
    g4 = weights[5, p] * (here - shift_z(after, 1))
    g5 = weights[6, p] * (here - shift_z(after, -1))
    leaving = (g1 + g2) + (g3 + g4) + g5
    arriving = (g1 + shift_y(g2, -1)) + (shift_y(g3, 1) + shift_z(g4, -1)) + shift_z(g5, 1)
    return leaving, arriving


def within(here, weights, p):
    up = shift_y(here, 1)
    h1 = weights[1, p] * (here - up)
    h2 = weights[2, p] * (here - shift_z(here, 1))
    h3 = weights[7, p] * (here - shift_z(up, 1))
    h4 = weights[8, p] * (here - shift_z(up, -1))
    back = shift_y(h1 + shift_z(h3, -1) + shift_z(h4, 1), -1) + shift_z(h2, -1)
    return (h1 + h2) + (h3 + h4) - back


def operate(plane, weights, low, high, emit):
    _, arriving = across(plane(low - 1), plane(low), weights, low - 1)
    for p in range(low, high):
        here = plane(p)
        leaving, coming = across(here, plane(p + 1), weights, p)
        emit(p, within(here, weights, p) + leaving - arriving)
        arriving = coming


def column_of(inverse, row):
    return jnp.sum(inverse * row, axis=1, keepdims=True)


def spread_planes(column, ids_ref):
    coarse = column.shape[0]
    wide = jnp.broadcast_to(column, (coarse, EZ))
    label = row_ids((coarse, EZ))
    row = row_ids((EY, EZ))
    cy = EY - 8
    planes = []
    for a in range(3):
        before, own, after = (
            jnp.sum(jnp.where(ids_ref[3 * a + b : 3 * a + b + 1, :] == label, wide, 0.0), axis=0, keepdims=True)
            for b in range(3)
        )
        planes.append(jnp.where(row < cy, own, jnp.where(row < cy + 4, after, before)))
    return planes


def by_plane(planes, cx):
    return lambda p: planes[0] if p < HALO else planes[1] if p < HALO + cx else planes[2]


def labelled_row(totals, norm, cross, ids_ref):
    lane = lane_ids((1, LANES))
    block = LANES // ZBLK
    row = jnp.where(lane == COARSE, jnp.sum(norm, keepdims=True).reshape(1, 1), 0.0)
    row = row + jnp.where(lane == COARSE + 1, jnp.sum(cross, keepdims=True).reshape(1, 1), 0.0)
    for j in range(ZBLK):
        total = jnp.sum(jnp.where(lane // block == j, totals, 0.0), axis=1, keepdims=True)
        label = ids_ref[4:5, j * block : j * block + 1]
        row = row + jnp.where(lane == label, total, 0.0)
    return row


def own_part(plane, cy, cz):
    return plane[:cy, :cz]


def coarse_kernel(rows_ref, ids_ref, near_ref, inverse_ref, rhs_ref):
    count = rows_ref.shape[0] * rows_ref.shape[1]
    flat = rows_ref[...].reshape(count, LANES)
    features = flat.T
    coarse = inverse_ref.shape[0]
    label = row_ids((coarse, count))
    slot_row = row_ids((SLOTS, count))
    packed = None
    for g in range(LANES // SLOTS):
        part = features[g * SLOTS : (g + 1) * SLOTS]
        reach = None
        for s in range(NNB):
            term = jnp.where(near_ref[g, s : s + 1, :] == label, part[s : s + 1], 0.0)
            reach = term if s == 0 else reach + term
        crossing = jnp.sum(jnp.where(slot_row < NNB, part, 0.0), axis=0, keepdims=True)
        sub = row_ids((8, count))
        extra = jnp.where(sub == 0, crossing, jnp.where(sub == 1, part[RHS_SLOT : RHS_SLOT + 1], 0.0))
        own = jnp.where(ids_ref[g : g + 1, :] == label, 1.0, 0.0)
        product = lax.dot_general(
            jnp.concatenate([reach, extra], axis=0), own, (((1,), (1,)), ((), ())),
            precision=HIGHEST, preferred_element_type=jnp.float32,
        )
        packed = product if g == 0 else packed + product
    coupling = packed[:coarse]
    mirrored = coupling.T
    row = row_ids((coarse, coarse))
    lane = lane_ids((coarse, coarse))
    diagonal = packed[coarse : coarse + 1] + jnp.sum(mirrored, axis=0, keepdims=True)
    matrix = jnp.where(row == lane, diagonal, 0.0) - (coupling + mirrored)
    for k in range(coarse):
        pivot_row = matrix[k : k + 1, :]
        column = matrix[:, k : k + 1]
        scaled = pivot_row / matrix[k : k + 1, k : k + 1]
        inverse_pivot = 1.0 / matrix[k : k + 1, k : k + 1]
        rest = matrix - column * scaled
        rest = jnp.where(lane == k, -column * inverse_pivot, rest)
        scaled = jnp.where(lane[k : k + 1] == k, inverse_pivot, scaled)
        matrix = jnp.where(row == k, scaled, rest)
    inverse_ref[...] = jnp.concatenate([matrix, jnp.zeros((coarse, LANES - coarse), jnp.float32)], axis=1)
    rhs_ref[...] = jnp.concatenate(
        [packed[coarse + 1 : coarse + 2], jnp.zeros((1, LANES - coarse), jnp.float32)], axis=1
    )


def first_kernel(weights_ref, source_ref, scale_ref, ids_ref, inverse_ref, rhs_ref,
                 residual_ref, image_ref, row_ref, column_ref):
    planes = source_ref.shape[0]
    cx, cy, cz = planes - 2 * HALO, EY - 8, LANES
    column = column_of(inverse_ref[...], rhs_ref[...])
    column_ref[...] = jnp.broadcast_to(column, column_ref.shape)
    residual_ref[0] = jnp.zeros((EY, EZ), jnp.float32)
    residual_ref[planes - 1] = jnp.zeros((EY, EZ), jnp.float32)

    def residual(p, image):
        residual_ref[p] = jnp.where(scale_ref[p] != 0.0, source_ref[p] - image, 0.0)

    operate(by_plane(spread_planes(column, ids_ref), cx), weights_ref, 1, planes - 1, residual)
    sums = [jnp.zeros((cy, cz), jnp.float32)] * 3

    def image(p, value):
        image_ref[p] = value
        if HALO <= p < HALO + cx:
            mine, field = own_part(value, cy, cz), own_part(residual_ref[p], cy, cz)
            sums[0] = sums[0] + mine
            sums[1] = sums[1] + field * field
            sums[2] = sums[2] + field * mine

    operate(lambda p: residual_ref[p], weights_ref, 2, planes - 2, image)
    row = labelled_row(jnp.sum(sums[0], axis=0, keepdims=True), sums[1], sums[2], ids_ref)
    row_ref[...] = jnp.broadcast_to(row.reshape(1, 1, LANES), row_ref.shape)


def second_kernel(weights_ref, scale_ref, residual_ref, image_ref, ids_ref, inverse_ref, sums_ref,
                  next_ref, product_ref, along_ref, row_ref, column_ref, scalars_ref, field_ref):
    planes = scale_ref.shape[0]
    cx, cy, cz = planes - 2 * HALO, EY - 8, LANES
    totals = jnp.sum(sums_ref[...], axis=0)
    column = column_of(inverse_ref[...], totals)
    column_ref[...] = jnp.broadcast_to(column, column_ref.shape)
    correction = jnp.sum(inverse_ref[...] * column, axis=0, keepdims=True)
    lane = lane_ids((1, LANES))
    inverse = inverse_ref[...]
    bent = jnp.sum(column * jnp.sum(jnp.where(lane_ids(inverse.shape) == row_ids(inverse.shape), totals, 0.0), axis=1, keepdims=True), axis=0, keepdims=True)
    norm = jnp.sum(jnp.where(lane == COARSE, totals, 0.0), axis=1, keepdims=True)
    cross = jnp.sum(jnp.where(lane == COARSE + 1, totals, 0.0), axis=1, keepdims=True)
    step = norm / (cross - bent)
    sub = row_ids((8, LANES))
    scalars_ref[...] = jnp.where(sub == 0, norm, jnp.where(sub == 1, step, 0.0))

    def follow(p, value):
        value = image_ref[p] - value
        if HALO <= p < HALO + cx:
            along_ref[p - HALO] = own_part(value, cy, cz)
        updated = jnp.where(scale_ref[p] != 0.0, residual_ref[p] - step * value, 0.0)
        field_ref[p] = updated
        if HALO <= p < HALO + cx:
            next_ref[p - HALO] = own_part(updated, cy, cz)

    operate(by_plane(spread_planes(column, ids_ref), cx), weights_ref, 2, planes - 2, follow)
    sums = [jnp.zeros((cy, cz), jnp.float32)] * 3

    def image(p, value):
        mine, field = own_part(value, cy, cz), own_part(field_ref[p], cy, cz)
        product_ref[p - HALO] = mine
        sums[0] = sums[0] + mine
        sums[1] = sums[1] + field * field
        sums[2] = sums[2] + field * mine

    operate(lambda p: field_ref[p], weights_ref, HALO, planes - HALO, image)
    row = labelled_row(jnp.sum(sums[0], axis=0, keepdims=True), sums[1], sums[2], ids_ref)
    row_ref[...] = jnp.broadcast_to(row.reshape(1, 1, LANES), row_ref.shape)


def last_kernel(weights_ref, residual_ref, next_ref, product_ref, along_ref, ids_ref, inverse_ref, sums_ref,
                scalars_ref, first_ref, second_ref, solution_ref, final_ref):
    cx, cy, cz = next_ref.shape
    planes = cx + 2 * HALO
    totals = jnp.sum(sums_ref[...], axis=0)
    inverse = inverse_ref[...]
    column = column_of(inverse, totals)
    lane = lane_ids((1, LANES))
    bent = jnp.sum(column * jnp.sum(jnp.where(lane_ids(inverse.shape) == row_ids(inverse.shape), totals, 0.0), axis=1, keepdims=True), axis=0, keepdims=True)
    norm = jnp.sum(jnp.where(lane == COARSE, totals, 0.0), axis=1, keepdims=True)
    cross = jnp.sum(jnp.where(lane == COARSE + 1, totals, 0.0), axis=1, keepdims=True)
    norm_before = scalars_ref[0:1, 0:1]
    step_before = scalars_ref[1:2, 0:1]
    ratio = norm / norm_before
    step = norm / (cross - bent - ratio * norm / step_before)
    kept = first_ref[:, 0:1] - step_before * second_ref[:, 0:1] - step * (column + ratio * second_ref[:, 0:1])
    coarse = own_part(spread_planes(kept, ids_ref)[1], cy, cz)

    def finish(p, value):
        at = p - HALO
        before = own_part(residual_ref[p], cy, cz)
        now = next_ref[at]
        along = product_ref[at] - own_part(value, cy, cz) + ratio * along_ref[at]
        final_ref[at] = now - step * along
        solution_ref[at] = coarse + step_before * before + step * (now + ratio * before)

    operate(by_plane(spread_planes(column, ids_ref), cx), weights_ref, HALO, planes - HALO, finish)


def call(kernel, name, outs, args, specs=None, scratch=()):
    return pl.pallas_call(
        kernel,
        name=name,
        out_shape=[jax.ShapeDtypeStruct(shape, jnp.float32) for shape in outs],
        in_specs=specs or [VMEM] * len(args),
        out_specs=[VMEM] * len(outs),
        scratch_shapes=[pltpu.VMEM(shape, jnp.float32) for shape in scratch],
    )(*args)


def both_sides(cells, axis, dim, width):
    count = lax.axis_size(axis)
    size = cells.shape[dim]
    head = lax.slice_in_dim(cells, 0, width, axis=dim)
    tail = lax.slice_in_dim(cells, size - width, size, axis=dim)
    before = lax.ppermute(tail, axis, [(i, i + 1) for i in range(count - 1)])
    after = lax.ppermute(head, axis, [(i + 1, i) for i in range(count - 1)])
    return before, after


def exchanged(rows, axes):
    return lax.all_to_all(rows, axes, 0, 0)


def summed(rows, gxy):
    row = jnp.sum(exchanged(rows, "gz"), axis=0, keepdims=True)
    return exchanged(jnp.broadcast_to(row, (gxy, 1, LANES)), ("gx", "gy"))


def body(right_side, fiber_class, conductivity_scale, class_tensor, block_ids):
    cx, cy, cz = right_side.shape
    gx, gy, gz = (lax.axis_size(a) for a in ("gx", "gy", "gz"))
    gxy, half = gx * gy, gz // 2
    place_x, place_y, place_z = (lax.axis_index(a) for a in ("gx", "gy", "gz"))

    (rows,) = call(
        own_sums_kernel, "own_sums", [(gz, 1, LANES)],
        [class_tensor, right_side, fiber_class, conductivity_scale, jnp.asarray(crossing_table())],
        specs=[SMEM, VMEM, VMEM, VMEM, VMEM], scratch=[(ROWS, cz)],
    )
    rows = exchanged(rows, "gz").reshape(gz, LANES)[:, : ZBLK * SLOTS]
    rows = jnp.concatenate([rows[:half], rows[half:]], axis=1)
    rows = exchanged(jnp.broadcast_to(rows[None], (gxy, half, LANES)), ("gx", "gy"))

    padded_ids = jnp.pad(block_ids, 1, constant_values=-1)
    shown = jnp.stack(
        [padded_ids[1 + a : 1 + a + gx, 1 + b : 1 + b + gy, 1 + c : 1 + c + gz * ZBLK] for a, b, c in ((0, 0, 0),) + NEIGHBOURS]
    )
    shown = shown.reshape(NNB + 1, gxy, 2, half, ZBLK)
    shown = jnp.transpose(shown, (2, 4, 0, 1, 3)).reshape(2 * ZBLK, NNB + 1, gxy * half)
    ids_all, near = shown[:, 0], shown[:, 1:]
    window = lax.dynamic_slice(padded_ids, (place_x, place_y, place_z * ZBLK), (3, 3, ZBLK + 2)).reshape(9, ZBLK + 2)
    block = cz // ZBLK
    ids = jnp.concatenate(
        [jnp.broadcast_to(window[:, 1 + j : 2 + j], (9, block)) for j in range(ZBLK)]
        + [
            jnp.broadcast_to(window[:, ZBLK + 1 :], (9, HALO)),
            jnp.full((9, EZ - cz - 2 * HALO), -1, jnp.int32),
            jnp.broadcast_to(window[:, :1], (9, HALO)),
        ],
        axis=1,
    )

    stacked = jnp.stack([right_side, fiber_class.astype(jnp.float32), conductivity_scale])
    before, after = both_sides(stacked, "gx", 1, HALO)
    stacked = jnp.concatenate([before, stacked, after], axis=1)
    before, after = both_sides(stacked, "gy", 2, HALO)
    gap = jnp.zeros((3, cx + 2 * HALO, EY - cy - 2 * HALO, cz), jnp.float32)
    stacked = jnp.concatenate([stacked, after, gap, before], axis=2)
    before, after = both_sides(stacked, "gz", 3, HALO)
    gap = jnp.zeros((3, cx + 2 * HALO, EY, EZ - cz - 2 * HALO), jnp.float32)
    stacked = jnp.concatenate([stacked, after, gap, before], axis=3)
    source, kinds, scale = stacked[0], stacked[1].astype(jnp.int32), stacked[2]
    extended = source.shape
    (weights,) = call(
        weights_kernel, "weights", [(len(EDGES),) + extended], [class_tensor, kinds, scale],
        specs=[SMEM, VMEM, VMEM], scratch=[(6,) + extended],
    )

    inverse, rhs = call(coarse_kernel, "coarse", [(COARSE, LANES), (1, LANES)], [rows, ids_all, near])
    residual, image, rows, first = call(
        first_kernel, "first", [extended, extended, (gz, 1, LANES), (COARSE, LANES)],
        [weights, source, scale, ids, inverse, rhs],
    )
    sums = summed(rows, gxy)
    following, product, along, rows, second, scalars = call(
        second_kernel, "second",
        [(cx, cy, cz)] * 3 + [(gz, 1, LANES), (COARSE, LANES), (8, LANES)],
        [weights, scale, residual, image, ids, inverse, sums],
        scratch=[extended],
    )
    sums = summed(rows, gxy)
    answer, final = call(
        last_kernel, "last", [(cx, cy, cz)] * 2,
        [weights, residual, following, product, along, ids, inverse, sums, scalars, first, second],
    )
    return answer, final


def solution(mesh):
    spec = P("gx", "gy", "gz")
    return jax.shard_map(
        body,
        mesh=mesh,
        in_specs=(spec, spec, spec, P(), P()),
        out_specs=(spec, spec),
        check_vma=False,
    )
```

time: 373 us -> 148 us (0.40)
  blocking collectives: 230 us -> 53.1 us
  Pallas kernels: 0 us -> 30.8 us
  starting transfers between devices: 69.8 us -> 41.3 us
  other arithmetic: 22.8 us -> 3.16 us
  matrix products: 14.2 us -> 0 us
  waiting for transfers between devices: 17.2 us -> 4.33 us
  between operations: 8.21 us -> 1.03 us
  local copies, waits for them, and re-layouts: 9.17 us -> 13 us
    psum x16 -> x0, blocking collectives: 230 us -> none  [over_axes(): return functools.reduce(lax.psum, axes, shard)]
    ppermute x24 -> x6, starting transfers between devices: 69.8 us -> 16 us  [the longest x3 9.95 us: both_sides(): before = lax.ppermute(tail, axis, [(i, i + 1) for i in range(count - 1)])]
    all_to_all x0 -> x4, blocking collectives: none -> 53.1 us  [exchanged(): return lax.all_to_all(rows, axes, 0, 0)]
    pallas_call x0 -> x6, Pallas kernels: none -> 30.8 us  [call(): pl.pallas_call(kernel, name=name, out_shape=[jax.ShapeDtypeStruct(shape,...]
    all_to_all x0 -> x2, starting transfers between devices: none -> 25.4 us  [exchanged(): return lax.all_to_all(rows, axes, 0, 0)]
    ppermute x24 -> x6, waiting for transfers between devices: 17.2 us -> 1.49 us  [the longest x3 1.2 us: both_sides(): before = lax.ppermute(tail, axis, [(i, i + 1) for i in range(count - 1)])]
    dot_general x66 -> x0, matrix products: 11.7 us -> none  [the longest x54 8.59 us: body(): jnp.einsum('xyz,xa,yb,zjc->jabc', weight, reach_onehot(CX, step_x), reach...]
    another operation x6 -> x1, other arithmetic: 12.1 us -> 0.84 us  [body(): jnp.stack([right_side, fiber_class.astype(jnp.float32), conductivity_scale])]
  transfers between devices with their start and end apart: 24 -> 8, of which waited for: 13 -> 3; matrix products, arithmetic and copies ran while one was open for 1% -> 10% of each run, Pallas kernels for 0% -> 4%
where the time goes in v1:
time: 148 us; the launch traced here: 147 us
  blocking collectives  53.1 us (36%)
  starting transfers between devices  41.3 us (28%)
  Pallas kernels  30.8 us (21%)
  local copies, waits for them, and re-layouts  13 us (9%)
  waiting for transfers between devices  4.33 us (3%)
  other arithmetic  3.16 us (2%)
    all_to_all x4, blocking collectives, exchanged(): return lax.all_to_all(rows, axes, 0, 0)  53.1 us
    pallas_call x6, Pallas kernels, call(): pl.pallas_call(kernel, name=name, out_shape=[jax.ShapeDtypeStruct(shape,...  30.8 us
    all_to_all x2, starting transfers between devices, exchanged(): return lax.all_to_all(rows, axes, 0, 0)  25.4 us
    ppermute x3, starting transfers between devices, both_sides(): before = lax.ppermute(tail, axis, [(i, i + 1) for i in range(count - 1)])  9.95 us
    ppermute x3, starting transfers between devices, both_sides(): after = lax.ppermute(head, axis, [(i + 1, i) for i in range(count - 1)])  6.01 us
    slice x19, local copies, waits for them, and re-layouts, body(): padded_ids[1 + a:1 + a + gx, 1 + b:1 + b + gy, 1 + c:1 + c + gz * ZBLK]  4.07 us
    unnamed x31, local copies, waits for them, and re-layouts  3.66 us
  transfers between devices with their start and end apart: 8, of which 3 were waited for; matrix products, arithmetic and copies ran while one was open for 10% of the time, Pallas kernels for 4%

profile of v1, /device:TPU:1, one launch (start us, length us, event | category | flops | bytes accessed | tf_op | source)
XLA Modules:
  0.0 146.8 jit_solution(14061087118660736980)
XLA Ops:
  0.6 2.3 %own_sums.1 = f32[16,1,128]{2,1,0:T(1,128)} custom-call(f32[6,16]{1,0:T(8,128)} %table_ref.3, f32[8,16,128]{2,1,0:T(8,128)} %source_ref.1, s32[8,16,128]{2,1,0:T(8,128)} %kinds_ref.1, f32[8,16,128]{2,1,0:T(8,128)} %scale_ref.1, f32[96,56]{1,0:T(8,128)} %constant.34.clone.crossing_ref), custom_call_target="tpu_custom_call" | custom-call | tf_op jit(solution)/shard_map/own_sums/pallas_call | solution.py:389
  3.0 10.1 %all-to-all-start = ((f32[16,1,128]{2,1,0:T(1,128)}), f32[16,1,128]{2,1,0:T(1,128)S(1)}, u32[]{:S(2)}, u32[]{:S(2)}) async-start(f32[16,1,128]{2,1,0:T(1,128)} %own_sums.1), calls=%async_computation | async-start | bytes 16384 | tf_op jit(solution)/shard_map/all_to_all | solution.py:410
  13.1 0.8 convert_bitcast_fusion
  13.9 0.8 pad_maximum_fusion.9
  14.7 2.5 %collective-permute-start = (f32[3,3,16,128]{3,2,1,0:T(8,128)S(1)}, f32[3,3,16,128]{3,2,1,0:T(8,128)S(1)}, u32[]{:S(2)}, u32[]{:S(2)}) collective-permute-start(f32[3,3,16,128]{3,2,1,0:T(8,128)S(1)} %get-tuple-element.33), channel_id=1, source_target_pairs={{0,64},{64,128},{128,192},{192,256},{256,320},{320,384},{384,448},... | collective-permute-start | bytes 221192 | tf_op jit(solution)/shard_map/ppermute | solution.py:404
  17.2 1.3 collective-permute-start.1
  18.5 0.9 copy.29
  19.4 1.5 %pad_slice_fusion = (s32[8,4,32]{2,1,0:T(4,128)S(1)}, s32[8,4,32]{2,1,0:T(4,128)S(1)}, s32[8,4,32]{2,1,0:T(4,128)S(1)}, s32[8,4,32]{2,1,0:T(4,128)S(1)}, s32[8,4...) fusion(s32[8,4,32]{2,1,0:T(4,128)} %param.10), kind=kLoop, calls=%fused_computation.6 | loop fusion | bytes 77824 | tf_op jit(solution)/shard_map/slice | solution.py:435
  20.9 0.8 pad_dynamic-slice_fusion
  22.3 0.1 copy.47
  22.5 0.1 copy.30
  22.8 0.1 copy.31
  23.0 0.1 copy.32
  23.3 0.1 copy.33
  23.5 0.1 copy.34
  23.8 0.1 copy.35
  24.0 0.1 copy.36
  24.3 0.1 copy.37
  24.6 0.1 copy.38
  24.8 0.1 copy.39
  25.1 0.1 copy.40
  27.1 0.3 copy.48
  27.4 0.2 slice.156
  27.6 0.8 copy.56
  28.4 0.8 copy.57.near_ref
  29.6 0.7 concatenate.19.ids_ref
  30.3 1.3 collective-permute-start.2
  31.6 4.0 %collective-permute-start.3 = (f32[3,14,3,128]{3,2,1,0:T(4,128)S(1)}, f32[3,14,3,128]{3,2,1,0:T(4,128)S(1)}, u32[]{:S(2)}, u32[]{:S(2)}) collective-permute-start(f32[3,14,3,128]{3,2,1,0:T(4,128)S(1)} %get-tuple-element.32), channel_id=1, source_target_pairs={{0,16},{16,32},{32,48},{1,17},{17,33},{33,49},{2,18},{18,34},{34,5... | collective-permute-start | bytes 193544 | tf_op jit(solution)/shard_map/ppermute | solution.py:404
  35.7 0.3 collective-permute-done.2
  35.9 1.2 collective-permute-done.3
  37.2 0.2 fusion.1
  37.4 3.4 %collective-permute-start.4 = (f32[3,14,24,3]{3,2,1,0:T(8,128)S(1)}, f32[3,14,24,3]{3,2,1,0:T(8,128)S(1)}, u32[]{:S(2)}, u32[]{:S(2)}) collective-permute-start(f32[3,14,24,3]{3,2,1,0:T(8,128)S(1)} %get-tuple-element.29), channel_id=1, source_target_pairs={{1,0},{2,1},{3,2},{4,3},{5,4},{6,5},{7,6},{8,7},{9,8},{10,9},{11,1... | collective-permute-start | bytes 36296 | tf_op jit(solution)/shard_map/ppermute | solution.py:405
  40.9 3.4 %collective-permute-start.5 = (f32[3,14,24,3]{3,2,1,0:T(8,128)S(1)}, f32[3,14,24,3]{3,2,1,0:T(8,128)S(1)}, u32[]{:S(2)}, u32[]{:S(2)}) collective-permute-start(f32[3,14,24,3]{3,2,1,0:T(8,128)S(1)} %get-tuple-element.30), channel_id=1, source_target_pairs={{0,1},{1,2},{2,3},{3,4},{4,5},{5,6},{6,7},{7,8},{8,9},{9,10},{10,1... | collective-permute-start | bytes 36296 | tf_op jit(solution)/shard_map/ppermute | solution.py:404
  44.4 0.7 broadcast_in_dim.66
  45.1 15.3 %all-to-all-start.1 = ((f32[32,8,128]{2,1,0:T(8,128)}), f32[32,8,128]{2,1,0:T(8,128)S(1)}, u32[]{:S(2)}, u32[]{:S(2)}) async-start(f32[32,8,128]{2,1,0:T(8,128)} %broadcast_in_dim.66), calls=%async_computation.1 | async-start | bytes 262144 | tf_op jit(solution)/shard_map/all_to_all | solution.py:410
  60.4 0.2 pad_maximum_fusion
  60.6 1.0 slice_bitcast_fusion
  61.6 6.4 %weights.1.weights_ref = f32[9,14,24,256]{3,2,1,0:T(8,128)} custom-call(f32[6,16]{1,0:T(8,128)} %table_ref.3, s32[14,24,256]{2,1,0:T(8,128)} %get-tuple-element.28.kinds_ref, f32[14,24,256]{2,1,0:T(8,128)} %get-tuple-element.27.scale_ref), custom_call_target="tpu_custom_call" | custom-call | tf_op jit(solution)/shard_map/weights/pallas_call | solution.py:389
  68.0 2.8 %all-to-all-done.1.rows_ref = f32[32,8,128]{2,1,0:T(8,128)S(1)} async-done(((f32[32,8,128]{2,1,0:T(8,128)}), f32[32,8,128]{2,1,0:T(8,128)S(1)}, u32[]{:S(2)}, u32[]{:S(2)}) %all-to-all-start.1) | async-done | bytes 131104 | tf_op jit(solution)/shard_map/all_to_all | solution.py:410
  70.9 0.7 copy-done.2
  71.5 8.4 %coarse.1 = (f32[64,128]{1,0:T(8,128)}, f32[1,128]{1,0:T(1,128)}) custom-call(f32[32,8,128]{2,1,0:T(8,128)} %copy-done.2, s32[4,256]{1,0:T(4,128)} %bitcast.69, s32[4,18,256]{2,1,0:T(8,128)} %copy.57.near_ref), custom_call_target="tpu_custom_call" | custom-call | tf_op jit(solution)/shard_map/coarse/pallas_call | solution.py:389
  80.0 5.5 %first.1 = (f32[14,24,256]{2,1,0:T(8,128)}, f32[14,24,256]{2,1,0:T(8,128)}, f32[16,1,128]{2,1,0:T(1,128)}, f32[64,128]{1,0:T(8,128)}) custom-call(f32[9,14,24,256]{3,2,1,0:T(8,128)} %weights.1.weights_ref, f32[14,24,256]{2,1,0:T(8,128)} %get-tuple-element.26.source_ref, f32[14,24,256]{2,1,0:T(8,128)} %get-tuple-element.27.scale_ref, ...), custom_call_target="tpu_custom_call" | custom-call | tf_op jit(solution)/shard_map/first/pallas_call | solution.py:389
  85.5 13.6 %all_to_all.30 = f32[16,1,128]{2,1,0:T(1,128)S(1)} all-to-all(f32[16,1,128]{2,1,0:T(1,128)} %get-tuple-element.18), channel_id=1, replica_groups=mesh['gx'=8,'gy'=4,'gz'=16] {'gz'}, dimensions={0} | all-to-all | bytes 16384 | tf_op jit(solution)/shard_map/all_to_all | solution.py:410
  99.2 14.7 %all_to_all.31.sums_ref = f32[32,1,128]{2,1,0:T(1,128)} all-to-all(f32[32,1,128]{2,1,0:T(1,128)S(1)} %broadcast_in_dim.67), channel_id=1, replica_groups=mesh['gx'=8,'gy'=4,'gz'=16] {'gx','gy'}, dimensions={0} | all-to-all | bytes 32768 | tf_op jit(solution)/shard_map/all_to_all | solution.py:410
  113.9 4.8 %second.1 = (f32[8,16,128]{2,1,0:T(8,128)}, f32[8,16,128]{2,1,0:T(8,128)}, f32[8,16,128]{2,1,0:T(8,128)}, f32[16,1,128]{2,1,0:T(1,128)}, f32[64,128]{1,0:T(8,128)}, /*index=5*/f32[8,128]{1,0:T(8,128)}) custom-call(f32[9,14,24,256]{3,2,1,0:T(8,128)} %weights.1.weights_ref, f32[14,24,256]{2,1,0:T(8,128)} %get-tuple-element.27.scale_ref, ...), custom_call_target="tpu_custom_call" | custom-call | tf_op jit(solution)/shard_map/second/pallas_call | solution.py:389
  118.7 12.5 %all_to_all.32 = f32[16,1,128]{2,1,0:T(1,128)S(1)} all-to-all(f32[16,1,128]{2,1,0:T(1,128)} %get-tuple-element.22), channel_id=1, replica_groups=mesh['gx'=8,'gy'=4,'gz'=16] {'gz'}, dimensions={0} | all-to-all | bytes 16384 | tf_op jit(solution)/shard_map/all_to_all | solution.py:410
  131.3 12.3 %all_to_all.33.sums_ref = f32[32,1,128]{2,1,0:T(1,128)} all-to-all(f32[32,1,128]{2,1,0:T(1,128)S(1)} %broadcast_in_dim.68), channel_id=1, replica_groups=mesh['gx'=8,'gy'=4,'gz'=16] {'gx','gy'}, dimensions={0} | all-to-all | bytes 32768 | tf_op jit(solution)/shard_map/all_to_all | solution.py:410
  143.5 3.3 %last.1 = (f32[8,16,128]{2,1,0:T(8,128)}, f32[8,16,128]{2,1,0:T(8,128)}) custom-call(f32[9,14,24,256]{3,2,1,0:T(8,128)} %weights.1.weights_ref, f32[14,24,256]{2,1,0:T(8,128)} %get-tuple-element.16.residual_ref, f32[8,16,128]{2,1,0:T(8,128)} %get-tuple-element.19.next_ref, f32[8,16,128]{2,1,0:T(8,128)} %get-tuple-element.20.product_ref, ...), custom_call_target="tpu_custom_call" | custom-call | tf_op jit(solution)/shard_map/last/pallas_call | solution.py:389
  (76 shorter events, 4.1 us)
Async XLA Ops:
  3.0 32.7 %all-to-all-start = ((f32[16,1,128]{2,1,0:T(1,128)}), f32[16,1,128]{2,1,0:T(1,128)S(1)}, u32[]{:S(2)}, u32[]{:S(2)}) async-start(f32[16,1,128]{2,1,0:T(1,128)} %own_sums.1), calls=%async_computation | async-start | bytes 16384 | tf_op jit(solution)/shard_map/all_to_all | solution.py:410
  14.7 15.6 %collective-permute-start = (f32[3,3,16,128]{3,2,1,0:T(8,128)S(1)}, f32[3,3,16,128]{3,2,1,0:T(8,128)S(1)}, u32[]{:S(2)}, u32[]{:S(2)}) collective-permute-start(f32[3,3,16,128]{3,2,1,0:T(8,128)S(1)} %get-tuple-element.33), channel_id=1, source_target_pairs={{0,64},{64,128},{128,192},{192,256},{256,320},{320,384},{384,448},... | collective-permute-start | bytes 221192 | tf_op jit(solution)/shard_map/ppermute | solution.py:404
  17.2 13.1 %collective-permute-start.1 = (f32[3,3,16,128]{3,2,1,0:T(8,128)S(1)}, f32[3,3,16,128]{3,2,1,0:T(8,128)S(1)}, u32[]{:S(2)}, u32[]{:S(2)}) collective-permute-start(f32[3,3,16,128]{3,2,1,0:T(8,128)S(1)} %get-tuple-element.34), channel_id=1, source_target_pairs={{64,0},{128,64},{192,128},{256,192},{320,256},{384,320},{448,384},... | collective-permute-start | bytes 221192 | tf_op jit(solution)/shard_map/ppermute | solution.py:405
  24.7 5.6 %copy-start = (f32[8,16,128]{2,1,0:T(8,128)S(1)}, f32[8,16,128]{2,1,0:T(8,128)}, u32[]{:S(2)}) copy-start(f32[8,16,128]{2,1,0:T(8,128)} %scale_ref.1) | copy-start | bytes 196612
  24.7 5.6 %copy-start.1 = (f32[8,16,128]{2,1,0:T(8,128)S(1)}, f32[8,16,128]{2,1,0:T(8,128)}, u32[]{:S(2)}) copy-start(f32[8,16,128]{2,1,0:T(8,128)} %source_ref.1) | copy-start | bytes 196612
  30.3 5.6 %collective-permute-start.2 = (f32[3,14,3,128]{3,2,1,0:T(4,128)S(1)}, f32[3,14,3,128]{3,2,1,0:T(4,128)S(1)}, u32[]{:S(2)}, u32[]{:S(2)}) collective-permute-start(f32[3,14,3,128]{3,2,1,0:T(4,128)S(1)} %get-tuple-element.31), channel_id=1, source_target_pairs={{16,0},{32,16},{48,32},{17,1},{33,17},{49,33},{18,2},{34,18},{50,3... | collective-permute-start | bytes 193544 | tf_op jit(solution)/shard_map/ppermute | solution.py:405
  31.6 5.5 %collective-permute-start.3 = (f32[3,14,3,128]{3,2,1,0:T(4,128)S(1)}, f32[3,14,3,128]{3,2,1,0:T(4,128)S(1)}, u32[]{:S(2)}, u32[]{:S(2)}) collective-permute-start(f32[3,14,3,128]{3,2,1,0:T(4,128)S(1)} %get-tuple-element.32), channel_id=1, source_target_pairs={{0,16},{16,32},{32,48},{1,17},{17,33},{33,49},{2,18},{18,34},{34,5... | collective-permute-start | bytes 193544 | tf_op jit(solution)/shard_map/ppermute | solution.py:404
  37.4 22.9 %collective-permute-start.4 = (f32[3,14,24,3]{3,2,1,0:T(8,128)S(1)}, f32[3,14,24,3]{3,2,1,0:T(8,128)S(1)}, u32[]{:S(2)}, u32[]{:S(2)}) collective-permute-start(f32[3,14,24,3]{3,2,1,0:T(8,128)S(1)} %get-tuple-element.29), channel_id=1, source_target_pairs={{1,0},{2,1},{3,2},{4,3},{5,4},{6,5},{7,6},{8,7},{9,8},{10,9},{11,1... | collective-permute-start | bytes 36296 | tf_op jit(solution)/shard_map/ppermute | solution.py:405
  40.9 19.5 %collective-permute-start.5 = (f32[3,14,24,3]{3,2,1,0:T(8,128)S(1)}, f32[3,14,24,3]{3,2,1,0:T(8,128)S(1)}, u32[]{:S(2)}, u32[]{:S(2)}) collective-permute-start(f32[3,14,24,3]{3,2,1,0:T(8,128)S(1)} %get-tuple-element.30), channel_id=1, source_target_pairs={{0,1},{1,2},{2,3},{3,4},{4,5},{5,6},{6,7},{7,8},{8,9},{9,10},{10,1... | collective-permute-start | bytes 36296 | tf_op jit(solution)/shard_map/ppermute | solution.py:404
  45.1 25.8 %all-to-all-start.1 = ((f32[32,8,128]{2,1,0:T(8,128)}), f32[32,8,128]{2,1,0:T(8,128)S(1)}, u32[]{:S(2)}, u32[]{:S(2)}) async-start(f32[32,8,128]{2,1,0:T(8,128)} %broadcast_in_dim.66), calls=%async_computation.1 | async-start | bytes 262144 | tf_op jit(solution)/shard_map/all_to_all | solution.py:410
  70.9 0.7 copy-start.2

commit v2 on v1

--- a/solution.py
+++ b/solution.py
@@ -100,8 +100,14 @@
     return lax.broadcasted_iota(jnp.int32, shape, len(shape) - 2)
 
 
-def own_sums_kernel(table_ref, source_ref, kinds_ref, scale_ref, crossing_ref, out_ref, rows_ref):
+def own_sums_kernel(table_ref, source_ref, kinds_ref, scale_ref, crossing_ref,
+                    out_ref, stacked_ref, head_ref, tail_ref, rows_ref):
     cx, cy, cz = source_ref.shape
+    for f, field in enumerate((source_ref, kinds_ref, scale_ref)):
+        cells = field[...].astype(jnp.float32)
+        stacked_ref[f] = cells
+        head_ref[f] = cells[:HALO]
+        tail_ref[f] = cells[cx - HALO :]
     rows_ref[...] = jnp.zeros_like(rows_ref)
     firsts, totals = None, None
     total_source = None
@@ -145,32 +151,98 @@
     return pltpu.roll(x, (-step) % EY, 0)
 
 
-def shift(x, step_y, step_z):
-    if step_y:
-        x = shift_y(x, step_y)
-    if step_z:
-        x = shift_z(x, step_z)
-    return x
-
-
-def weights_kernel(table_ref, kinds_ref, scale_ref, out_ref, layers_ref):
-    planes = scale_ref.shape[0]
-
-    def fill(p, carry):
-        for c, layer in enumerate(lookup(kinds_ref[p], scale_ref[p], table_ref)):
-            layers_ref[c, p] = layer
-        return carry
-
-    lax.fori_loop(0, planes, fill, 0)
-
-    def edges(p, carry):
-        after = jnp.minimum(p + 1, planes - 1)
-        for e, (sx, sy, sz, c, factor) in enumerate(EDGES):
-            beside = layers_ref[c, after] if sx else layers_ref[c, p]
-            out_ref[e, p] = (0.5 * factor) * (layers_ref[c, p] + shift(beside, sy, sz))
-        return carry
-
-    lax.fori_loop(0, planes, edges, 0)
+def widen_kernel(rows_ref, out_ref):
+    half = out_ref.shape[1]
+    rows = rows_ref[...].reshape(2 * half, LANES)
+    rows = rows[:half] + pltpu.roll(rows[half:], LANES // 2, 1)
+    out_ref[...] = jnp.broadcast_to(rows[None], out_ref.shape)
+
+
+def labels_kernel(block_ref, own_ref, near_ref, window_ref, flat_ref):
+    gx, gy, nz = block_ref.shape
+    gxy, half = gx * gy, nz // (2 * ZBLK)
+    count = gxy * half
+    for x in range(gx):
+        flat_ref[x * gy : (x + 1) * gy, :] = block_ref[x].astype(jnp.float32) + 1.0
+    flat = flat_ref[...]
+    lane = lane_ids((gxy, count))
+    row = row_ids((gxy, count))
+    lane_x, lane_y = lane // half // gy, lane // half % gy
+    depth = row_ids((nz, count))
+    lane_r = lane_ids((nz, count)) % half
+    own_ref[...] = jnp.zeros_like(own_ref)
+    near_ref[...] = jnp.zeros_like(near_ref)
+    for a in (-1, 0, 1):
+        for b in (-1, 0, 1):
+            steps = [c for c in (-1, 0, 1) if abs(a) + abs(b) + abs(c) <= 2]
+            hit = (row == (lane_x + a) * gy + lane_y + b) & (lane_x + a >= 0) & (lane_x + a < gx)
+            hit = hit & (lane_y + b >= 0) & (lane_y + b < gy)
+            columns = lax.dot_general(
+                flat, jnp.where(hit, 1.0, 0.0), (((0,), (0,)), ((), ())),
+                precision=HIGHEST, preferred_element_type=jnp.float32,
+            )
+            for g in range(2 * ZBLK):
+                level = ZBLK * (g // ZBLK * half + lane_r) + g % ZBLK
+                for c in steps:
+                    found = jnp.sum(jnp.where(depth == level + c, columns, 0.0), axis=0, keepdims=True)
+                    found = (found + 0.5).astype(jnp.int32) - 1
+                    if (a, b, c) == (0, 0, 0):
+                        own_ref[g : g + 1, :] = found
+                    else:
+                        s = NEIGHBOURS.index((a, b, c))
+                        near_ref[g, s : s + 1, :] = found
+    place_x, place_y, place_z = (lax.axis_index(n) for n in ("gx", "gy", "gz"))
+    at = row_ids((16, gxy))
+    beside_x, beside_y = place_x + at // 3 - 1, place_y + at % 3 - 1
+    hit = (lane_ids((16, gxy)) == beside_x * gy + beside_y) & (beside_x >= 0) & (beside_x < gx)
+    hit = hit & (beside_y >= 0) & (beside_y < gy) & (at < 9)
+    picked = jnp.dot(jnp.where(hit, 1.0, 0.0), flat, precision=HIGHEST, preferred_element_type=jnp.float32)
+    lane = lane_ids((nz, EZ))
+    level = ZBLK * place_z + jnp.where(
+        lane < LANES, lane // (LANES // ZBLK), jnp.where(lane < LANES + HALO, ZBLK, -1)
+    )
+    hit = (row_ids((nz, EZ)) == level) & ((lane < LANES + HALO) | (lane >= EZ - HALO))
+    window = jnp.dot(picked, jnp.where(hit, 1.0, 0.0), precision=HIGHEST, preferred_element_type=jnp.float32)
+    window_ref[...] = (window + 0.5).astype(jnp.int32) - 1
+
+
+def fill_weights(table_ref, stacked_ref, out_ref):
+    planes = stacked_ref.shape[1]
+
+    def layers_of(p):
+        layers = lookup(stacked_ref[1, p], stacked_ref[2, p], table_ref)
+        return [(0.5 if c < 3 else 0.25) * layer for c, layer in enumerate(layers)]
+
+    here = layers_of(0)
+    for p in range(planes):
+        after = layers_of(p + 1) if p + 1 < planes else here
+        up = shift_y(here[5], 1)
+        out_ref[0, p] = here[0] + after[0]
+        out_ref[1, p] = here[1] + shift_y(here[1], 1)
+        out_ref[2, p] = here[2] + shift_z(here[2], 1)
+        out_ref[3, p] = here[3] + shift_y(after[3], 1)
+        out_ref[4, p] = -(here[3] + shift_y(after[3], -1))
+        out_ref[5, p] = here[4] + shift_z(after[4], 1)
+        out_ref[6, p] = -(here[4] + shift_z(after[4], -1))
+        out_ref[7, p] = here[5] + shift_z(up, 1)
+        out_ref[8, p] = -(here[5] + shift_z(up, -1))
+        here = after
+
+
+def inside_mask(sides_ref):
+    row, lane = row_ids((EY, EZ)), lane_ids((EY, EZ))
+    cy = EY - 8
+    rows = (row < cy) | ((row < cy + HALO) & (sides_ref[3] > 0)) | ((row >= EY - HALO) & (sides_ref[2] > 0))
+    lanes = (lane < LANES) | ((lane < LANES + HALO) & (sides_ref[5] > 0)) | ((lane >= EZ - HALO) & (sides_ref[4] > 0))
+    return rows & lanes
+
+
+def inside_plane(mask, p, cx, sides_ref):
+    if p < HALO:
+        return mask & (sides_ref[0] > 0)
+    if p >= HALO + cx:
+        return mask & (sides_ref[1] > 0)
+    return mask
 
 
 def across(here, after, weights, p):
@@ -272,32 +344,41 @@
     lane = lane_ids((coarse, coarse))
     diagonal = packed[coarse : coarse + 1] + jnp.sum(mirrored, axis=0, keepdims=True)
     matrix = jnp.where(row == lane, diagonal, 0.0) - (coupling + mirrored)
-    for k in range(coarse):
-        pivot_row = matrix[k : k + 1, :]
-        column = matrix[:, k : k + 1]
-        scaled = pivot_row / matrix[k : k + 1, k : k + 1]
-        inverse_pivot = 1.0 / matrix[k : k + 1, k : k + 1]
-        rest = matrix - column * scaled
-        rest = jnp.where(lane == k, -column * inverse_pivot, rest)
-        scaled = jnp.where(lane[k : k + 1] == k, inverse_pivot, scaled)
-        matrix = jnp.where(row == k, scaled, rest)
+    panel = 8
+    for start in range(0, coarse, panel):
+        columns = [
+            jnp.broadcast_to(matrix[:, k : k + 1], (coarse, coarse)) for k in range(start, start + panel)
+        ]
+        for i in range(panel):
+            k = start + i
+            column = columns[i]
+            inverse_pivot = 1.0 / column[k : k + 1, :]
+            scaled = matrix[k : k + 1, :] * inverse_pivot
+            scaled = jnp.where(lane[:1] == k, inverse_pivot, scaled)
+            matrix = jnp.where(lane == k, 0.0, matrix) - column * scaled
+            matrix = jnp.where(row == k, scaled, matrix)
+            for m in range(i + 1, panel):
+                factor = columns[m][k : k + 1, :] * inverse_pivot
+                columns[m] = jnp.where(row == k, factor, columns[m] - column * factor)
     inverse_ref[...] = jnp.concatenate([matrix, jnp.zeros((coarse, LANES - coarse), jnp.float32)], axis=1)
     rhs_ref[...] = jnp.concatenate(
         [packed[coarse + 1 : coarse + 2], jnp.zeros((1, LANES - coarse), jnp.float32)], axis=1
     )
 
 
-def first_kernel(weights_ref, source_ref, scale_ref, ids_ref, inverse_ref, rhs_ref,
-                 residual_ref, image_ref, row_ref, column_ref):
-    planes = source_ref.shape[0]
+def first_kernel(table_ref, sides_ref, stacked_ref, ids_ref, inverse_ref, rhs_ref,
+                 weights_ref, residual_ref, image_ref, row_ref, column_ref):
+    planes = stacked_ref.shape[1]
     cx, cy, cz = planes - 2 * HALO, EY - 8, LANES
+    fill_weights(table_ref, stacked_ref, weights_ref)
+    mask = inside_mask(sides_ref)
     column = column_of(inverse_ref[...], rhs_ref[...])
     column_ref[...] = jnp.broadcast_to(column, column_ref.shape)
     residual_ref[0] = jnp.zeros((EY, EZ), jnp.float32)
     residual_ref[planes - 1] = jnp.zeros((EY, EZ), jnp.float32)
 
     def residual(p, image):
-        residual_ref[p] = jnp.where(scale_ref[p] != 0.0, source_ref[p] - image, 0.0)
+        residual_ref[p] = jnp.where(inside_plane(mask, p, cx, sides_ref), stacked_ref[0, p] - image, 0.0)
 
     operate(by_plane(spread_planes(column, ids_ref), cx), weights_ref, 1, planes - 1, residual)
     sums = [jnp.zeros((cy, cz), jnp.float32)] * 3
@@ -315,14 +396,14 @@
     row_ref[...] = jnp.broadcast_to(row.reshape(1, 1, LANES), row_ref.shape)
 
 
-def second_kernel(weights_ref, scale_ref, residual_ref, image_ref, ids_ref, inverse_ref, sums_ref,
+def second_kernel(sides_ref, weights_ref, residual_ref, image_ref, ids_ref, inverse_ref, sums_ref,
                   next_ref, product_ref, along_ref, row_ref, column_ref, scalars_ref, field_ref):
-    planes = scale_ref.shape[0]
+    planes = residual_ref.shape[0]
     cx, cy, cz = planes - 2 * HALO, EY - 8, LANES
+    mask = inside_mask(sides_ref)
     totals = jnp.sum(sums_ref[...], axis=0)
     column = column_of(inverse_ref[...], totals)
     column_ref[...] = jnp.broadcast_to(column, column_ref.shape)
-    correction = jnp.sum(inverse_ref[...] * column, axis=0, keepdims=True)
     lane = lane_ids((1, LANES))
     inverse = inverse_ref[...]
     bent = jnp.sum(column * jnp.sum(jnp.where(lane_ids(inverse.shape) == row_ids(inverse.shape), totals, 0.0), axis=1, keepdims=True), axis=0, keepdims=True)
@@ -336,7 +417,7 @@
         value = image_ref[p] - value
         if HALO <= p < HALO + cx:
             along_ref[p - HALO] = own_part(value, cy, cz)
-        updated = jnp.where(scale_ref[p] != 0.0, residual_ref[p] - step * value, 0.0)
+        updated = jnp.where(inside_plane(mask, p, cx, sides_ref), residual_ref[p] - step * value, 0.0)
         field_ref[p] = updated
         if HALO <= p < HALO + cx:
             next_ref[p - HALO] = own_part(updated, cy, cz)
@@ -385,22 +466,22 @@
     operate(by_plane(spread_planes(column, ids_ref), cx), weights_ref, HALO, planes - HALO, finish)
 
 
-def call(kernel, name, outs, args, specs=None, scratch=()):
+def call(kernel, outs, args, specs=None, scratch=()):
     return pl.pallas_call(
         kernel,
-        name=name,
-        out_shape=[jax.ShapeDtypeStruct(shape, jnp.float32) for shape in outs],
+        out_shape=[
+            shape if isinstance(shape, jax.ShapeDtypeStruct) else jax.ShapeDtypeStruct(shape, jnp.float32)
+            for shape in outs
+        ],
         in_specs=specs or [VMEM] * len(args),
         out_specs=[VMEM] * len(outs),
         scratch_shapes=[pltpu.VMEM(shape, jnp.float32) for shape in scratch],
+        compiler_params=pltpu.CompilerParams(vmem_limit_bytes=16 * 2**20),
     )(*args)
 
 
-def both_sides(cells, axis, dim, width):
+def both_sides(head, tail, axis):
     count = lax.axis_size(axis)
-    size = cells.shape[dim]
-    head = lax.slice_in_dim(cells, 0, width, axis=dim)
-    tail = lax.slice_in_dim(cells, size - width, size, axis=dim)
     before = lax.ppermute(tail, axis, [(i, i + 1) for i in range(count - 1)])
     after = lax.ppermute(head, axis, [(i + 1, i) for i in range(count - 1)])
     return before, after
@@ -419,67 +500,55 @@
     cx, cy, cz = right_side.shape
     gx, gy, gz = (lax.axis_size(a) for a in ("gx", "gy", "gz"))
     gxy, half = gx * gy, gz // 2
-    place_x, place_y, place_z = (lax.axis_index(a) for a in ("gx", "gy", "gz"))
-
-    (rows,) = call(
-        own_sums_kernel, "own_sums", [(gz, 1, LANES)],
+    slab = (3, HALO, cy, cz)
+    rows, stacked, head, tail = call(
+        own_sums_kernel, [(gz, 1, LANES), (3, cx, cy, cz), slab, slab],
         [class_tensor, right_side, fiber_class, conductivity_scale, jnp.asarray(crossing_table())],
         specs=[SMEM, VMEM, VMEM, VMEM, VMEM], scratch=[(ROWS, cz)],
     )
-    rows = exchanged(rows, "gz").reshape(gz, LANES)[:, : ZBLK * SLOTS]
-    rows = jnp.concatenate([rows[:half], rows[half:]], axis=1)
-    rows = exchanged(jnp.broadcast_to(rows[None], (gxy, half, LANES)), ("gx", "gy"))
-
-    padded_ids = jnp.pad(block_ids, 1, constant_values=-1)
-    shown = jnp.stack(
-        [padded_ids[1 + a : 1 + a + gx, 1 + b : 1 + b + gy, 1 + c : 1 + c + gz * ZBLK] for a, b, c in ((0, 0, 0),) + NEIGHBOURS]
-    )
-    shown = shown.reshape(NNB + 1, gxy, 2, half, ZBLK)
-    shown = jnp.transpose(shown, (2, 4, 0, 1, 3)).reshape(2 * ZBLK, NNB + 1, gxy * half)
-    ids_all, near = shown[:, 0], shown[:, 1:]
-    window = lax.dynamic_slice(padded_ids, (place_x, place_y, place_z * ZBLK), (3, 3, ZBLK + 2)).reshape(9, ZBLK + 2)
-    block = cz // ZBLK
-    ids = jnp.concatenate(
-        [jnp.broadcast_to(window[:, 1 + j : 2 + j], (9, block)) for j in range(ZBLK)]
-        + [
-            jnp.broadcast_to(window[:, ZBLK + 1 :], (9, HALO)),
-            jnp.full((9, EZ - cz - 2 * HALO), -1, jnp.int32),
-            jnp.broadcast_to(window[:, :1], (9, HALO)),
-        ],
-        axis=1,
-    )
-
-    stacked = jnp.stack([right_side, fiber_class.astype(jnp.float32), conductivity_scale])
-    before, after = both_sides(stacked, "gx", 1, HALO)
+    rows = exchanged(rows, "gz")
+    (rows,) = call(widen_kernel, [(gxy, half, LANES)], [rows])
+    rows = exchanged(rows, ("gx", "gy"))
+
+    whole = functools.partial(jax.ShapeDtypeStruct, dtype=jnp.int32)
+    ids_all, near, ids = call(
+        labels_kernel,
+        [whole((8, gxy * half)), whole((2 * ZBLK, 24, gxy * half)), whole((16, EZ))],
+        [block_ids], scratch=[(gxy, gz * ZBLK)],
+    )
+
+    before, after = both_sides(head, tail, "gx")
     stacked = jnp.concatenate([before, stacked, after], axis=1)
-    before, after = both_sides(stacked, "gy", 2, HALO)
+    before, after = both_sides(stacked[:, :, :HALO], stacked[:, :, cy - HALO :], "gy")
     gap = jnp.zeros((3, cx + 2 * HALO, EY - cy - 2 * HALO, cz), jnp.float32)
     stacked = jnp.concatenate([stacked, after, gap, before], axis=2)
-    before, after = both_sides(stacked, "gz", 3, HALO)
+    before, after = both_sides(stacked[..., :HALO], stacked[..., cz - HALO :], "gz")
     gap = jnp.zeros((3, cx + 2 * HALO, EY, EZ - cz - 2 * HALO), jnp.float32)
     stacked = jnp.concatenate([stacked, after, gap, before], axis=3)
-    source, kinds, scale = stacked[0], stacked[1].astype(jnp.int32), stacked[2]
-    extended = source.shape
-    (weights,) = call(
-        weights_kernel, "weights", [(len(EDGES),) + extended], [class_tensor, kinds, scale],
-        specs=[SMEM, VMEM, VMEM], scratch=[(6,) + extended],
-    )
-
-    inverse, rhs = call(coarse_kernel, "coarse", [(COARSE, LANES), (1, LANES)], [rows, ids_all, near])
-    residual, image, rows, first = call(
-        first_kernel, "first", [extended, extended, (gz, 1, LANES), (COARSE, LANES)],
-        [weights, source, scale, ids, inverse, rhs],
+    extended = stacked.shape[1:]
+    places = [lax.axis_index(a) for a in ("gx", "gy", "gz")]
+    sides = jnp.stack(
+        [jnp.int32(f) for place, count in zip(places, (gx, gy, gz)) for f in (place > 0, place < count - 1)]
+    )
+
+    inverse, rhs = call(coarse_kernel, [(COARSE, LANES), (1, LANES)], [rows, ids_all, near])
+    weights, residual, image, rows, first = call(
+        first_kernel,
+        [(len(EDGES),) + extended, extended, extended, (gz, 1, LANES), (COARSE, LANES)],
+        [class_tensor, sides, stacked, ids, inverse, rhs],
+        specs=[SMEM, SMEM, VMEM, VMEM, VMEM, VMEM],
     )
     sums = summed(rows, gxy)
     following, product, along, rows, second, scalars = call(
-        second_kernel, "second",
+        second_kernel,
         [(cx, cy, cz)] * 3 + [(gz, 1, LANES), (COARSE, LANES), (8, LANES)],
-        [weights, scale, residual, image, ids, inverse, sums],
+        [sides, weights, residual, image, ids, inverse, sums],
+        specs=[SMEM] + [VMEM] * 6,
         scratch=[extended],
     )
     sums = summed(rows, gxy)
     answer, final = call(
-        last_kernel, "last", [(cx, cy, cz)] * 2,
+        last_kernel, [(cx, cy, cz)] * 2,
         [weights, residual, following, product, along, ids, inverse, sums, scalars, first, second],
     )
     return answer, final

time: 148 us -> 137 us (0.926)
  Pallas kernels: 30.8 us -> 15.9 us
  waiting for transfers between devices: 4.33 us -> 12.5 us
  blocking collectives: 53.1 us -> 49.7 us
  starting transfers between devices: 41.3 us -> 38.3 us
  local copies, waits for them, and re-layouts: 13 us -> 15.6 us
    pallas_call x6 -> x7, Pallas kernels: 30.8 us -> 15.9 us  [call(): pl.pallas_call(kernel, out_shape=[shape if isinstance(shape, jax.ShapeDty...]
    unnamed x31 -> x46, local copies, waits for them, and re-layouts: 3.66 us -> 14.5 us
    all_to_all x2, waiting for transfers between devices: 2.84 us -> 8.1 us  [exchanged(): return lax.all_to_all(rows, axes, 0, 0)]
    slice x23 -> x2, local copies, waits for them, and re-layouts: 4.55 us -> 0.23 us  [the longest x1 0.2 us: body(): stacked[..., :HALO]]
    ppermute x3, waiting for transfers between devices: 0.29 us -> 4.33 us  [both_sides(): after = lax.ppermute(head, axis, [(i + 1, i) for i in range(count - 1)])]
    all_to_all x2, starting transfers between devices: 25.4 us -> 21.4 us  [exchanged(): return lax.all_to_all(rows, axes, 0, 0)]
    all_to_all x4, blocking collectives: 53.1 us -> 49.7 us  [exchanged(): return lax.all_to_all(rows, axes, 0, 0)]
    ppermute x3, starting transfers between devices: 9.95 us -> 12.3 us  [both_sides(): before = lax.ppermute(tail, axis, [(i, i + 1) for i in range(count - 1)])]
  transfers between devices with their start and end apart: 8 -> 8, of which waited for: 3 -> 4; matrix products, arithmetic and copies ran while one was open for 10% -> 1% of each run, Pallas kernels for 4% -> 1%
where the time goes in v2:
time: 137 us; the launch traced here: 136 us
  blocking collectives  49.7 us (36%)
  starting transfers between devices  38.3 us (28%)
  Pallas kernels  15.9 us (12%)
  local copies, waits for them, and re-layouts  15.6 us (11%)
  waiting for transfers between devices  12.5 us (9%)
  other arithmetic  2.63 us (2%)
    all_to_all x4, blocking collectives, exchanged(): return lax.all_to_all(rows, axes, 0, 0)  49.7 us
    all_to_all x2, starting transfers between devices, exchanged(): return lax.all_to_all(rows, axes, 0, 0)  21.4 us
    pallas_call x7, Pallas kernels, call(): pl.pallas_call(kernel, out_shape=[shape if isinstance(shape, jax.ShapeDty...  15.9 us
    unnamed x46, local copies, waits for them, and re-layouts  14.5 us
    ppermute x3, starting transfers between devices, both_sides(): before = lax.ppermute(tail, axis, [(i, i + 1) for i in range(count - 1)])  12.3 us
    all_to_all x2, waiting for transfers between devices, exchanged(): return lax.all_to_all(rows, axes, 0, 0)  8.1 us
    ppermute x3, starting transfers between devices, both_sides(): after = lax.ppermute(head, axis, [(i + 1, i) for i in range(count - 1)])  4.6 us
    ppermute x3, waiting for transfers between devices, both_sides(): after = lax.ppermute(head, axis, [(i + 1, i) for i in range(count - 1)])  4.33 us
  transfers between devices with their start and end apart: 8, of which 4 were waited for; matrix products, arithmetic and copies ran while one was open for 1% of the time, Pallas kernels for 1%

profile of v2, /device:TPU:1, one launch (start us, length us, event | category | flops | bytes accessed | tf_op | source)
XLA Modules:
  0.0 135.6 jit_solution(10823857114631481833)
XLA Ops:
  0.6 0.8 copy-done.7
  1.5 0.8 copy-done.8
  2.3 0.8 copy-done.9
  3.2 0.8 copy-done.10
  4.0 0.7 copy-done.15
  4.6 2.0 %shard_map.77 = (f32[16,1,128]{2,1,0:T(1,128)}, f32[3,8,16,128]{3,2,1,0:T(8,128)S(1)}, f32[3,3,16,128]{3,2,1,0:T(8,128)S(1)}, f32[3,3,16,128]{3,2,1,0:T(8,128)S(1)}) custom-call(f32[6,16]{1,0:T(8,128)S(1)} %copy-done.15, f32[8,16,128]{2,1,0:T(8,128)S(1)} %copy-done.7, s32[8,16,128]{2,1,0:T(8,128)S(1)} %copy-done.8, f32[8,16,128]{2,1,0:T(8,128)S(1)} %copy-done.9, ...), custom_call_target="tpu_custom_call" | custom-call | tf_op jit(solution)/shard_map/pallas_call | solution.py:470
  6.7 4.8 %collective-permute-start = (f32[3,3,16,128]{3,2,1,0:T(8,128)S(1)}, f32[3,3,16,128]{3,2,1,0:T(8,128)S(1)}, u32[]{:S(2)}, u32[]{:S(2)}) collective-permute-start(f32[3,3,16,128]{3,2,1,0:T(8,128)S(1)} %get-tuple-element.22), channel_id=1, source_target_pairs={{0,64},{64,128},{128,192},{192,256},{256,320},{320,384},{384,448},... | collective-permute-start | bytes 221192 | tf_op jit(solution)/shard_map/ppermute | solution.py:485
  11.5 1.3 collective-permute-start.1
  12.8 0.1 collective-permute-done
  12.9 4.3 %collective-permute-done.1 = f32[3,3,16,128]{3,2,1,0:T(8,128)S(1)} collective-permute-done((f32[3,3,16,128]{3,2,1,0:T(8,128)S(1)}, f32[3,3,16,128]{3,2,1,0:T(8,128)S(1)}, u32[]{:S(2)}, u32[]{:S(2)}) %collective-permute-start.1) | collective-permute-done | bytes 73760 | tf_op jit(solution)/shard_map/ppermute | solution.py:486
  17.3 1.3 collective-permute-start.2
  18.6 4.0 %collective-permute-start.3 = (f32[3,14,3,128]{3,2,1,0:T(4,128)S(1)}, f32[3,14,3,128]{3,2,1,0:T(4,128)S(1)}, u32[]{:S(2)}, u32[]{:S(2)}) collective-permute-start(f32[3,14,3,128]{3,2,1,0:T(4,128)S(1)} %get-tuple-element.45), channel_id=1, source_target_pairs={{0,16},{16,32},{32,48},{1,17},{17,33},{33,49},{2,18},{18,34},{34,5... | collective-permute-start | bytes 193544 | tf_op jit(solution)/shard_map/ppermute | solution.py:485
  22.6 9.5 %all-to-all-start = ((f32[16,1,128]{2,1,0:T(1,128)}), f32[16,1,128]{2,1,0:T(1,128)S(1)}, u32[]{:S(2)}, u32[]{:S(2)}) async-start(f32[16,1,128]{2,1,0:T(1,128)} %get-tuple-element.26), calls=%async_computation | async-start | bytes 16384 | tf_op jit(solution)/shard_map/all_to_all | solution.py:491
  32.1 0.1 pad_maximum_fusion.1
  32.2 0.2 fusion
  32.4 2.0 %collective-permute-start.4 = (f32[3,14,24,3]{3,2,1,0:T(8,128)S(1)}, f32[3,14,24,3]{3,2,1,0:T(8,128)S(1)}, u32[]{:S(2)}, u32[]{:S(2)}) collective-permute-start(f32[3,14,24,3]{3,2,1,0:T(8,128)S(1)} %get-tuple-element.42), channel_id=1, source_target_pairs={{1,0},{2,1},{3,2},{4,3},{5,4},{6,5},{7,6},{8,7},{9,8},{10,9},{11,1... | collective-permute-start | bytes 36296 | tf_op jit(solution)/shard_map/ppermute | solution.py:486
  34.4 3.5 %collective-permute-start.5 = (f32[3,14,24,3]{3,2,1,0:T(8,128)S(1)}, f32[3,14,24,3]{3,2,1,0:T(8,128)S(1)}, u32[]{:S(2)}, u32[]{:S(2)}) collective-permute-start(f32[3,14,24,3]{3,2,1,0:T(8,128)S(1)} %get-tuple-element.43), channel_id=1, source_target_pairs={{0,1},{1,2},{2,3},{3,4},{4,5},{5,6},{6,7},{7,8},{8,9},{9,10},{10,1... | collective-permute-start | bytes 36296 | tf_op jit(solution)/shard_map/ppermute | solution.py:485
  38.0 1.1 all-to-all-done.rows_ref
  39.0 0.7 shard_map.79
  39.8 11.9 %all-to-all-start.1 = ((f32[32,8,128]{2,1,0:T(8,128)}), f32[32,8,128]{2,1,0:T(8,128)S(1)}, u32[]{:S(2)}, u32[]{:S(2)}) async-start(f32[32,8,128]{2,1,0:T(8,128)} %shard_map.79), calls=%async_computation.1 | async-start | bytes 262144 | tf_op jit(solution)/shard_map/all_to_all | solution.py:491
  51.7 0.1 stack.35
  51.8 0.9 shard_map.78
  52.8 1.2 pad_maximum_fusion.stacked_ref
  54.0 7.0 %all-to-all-done.1.rows_ref = f32[32,8,128]{2,1,0:T(8,128)S(1)} async-done(((f32[32,8,128]{2,1,0:T(8,128)}), f32[32,8,128]{2,1,0:T(8,128)S(1)}, u32[]{:S(2)}, u32[]{:S(2)}) %all-to-all-start.1) | async-done | bytes 131104 | tf_op jit(solution)/shard_map/all_to_all | solution.py:491
  61.0 2.7 %shard_map.80 = (f32[64,128]{1,0:T(8,128)S(1)}, f32[1,128]{1,0:T(1,128)S(1)}) custom-call(f32[32,8,128]{2,1,0:T(8,128)S(1)} %all-to-all-done.1.rows_ref, s32[8,256]{1,0:T(8,128)S(1)} %get-tuple-element.27.ids_ref, s32[4,24,256]{2,1,0:T(8,128)S(1)} %get-tuple-element.28.near_ref), custom_call_target="tpu_custom_call" | custom-call | tf_op jit(solution)/shard_map/pallas_call | solution.py:470
  63.8 1.2 copy-done
  65.0 5.8 %shard_map.81 = (f32[9,14,24,256]{3,2,1,0:T(8,128)S(1)}, f32[14,24,256]{2,1,0:T(8,128)S(1)}, f32[14,24,256]{2,1,0:T(8,128)S(1)}, f32[16,1,128]{2,1,0:T(1,128)S(1)}, f32[64,128]{1,0:T(8,128)S(1)}) custom-call(f32[6,16]{1,0:T(8,128)S(1)} %copy-done.16, s32[6]{0:T(128)S(1)} %stack.36.sides_ref, f32[3,14,24,256]{3,2,1,0:T(8,128)S(1)} %copy-done, ...), custom_call_target="tpu_custom_call" | custom-call | tf_op jit(solution)/shard_map/pallas_call | solution.py:470
  70.7 0.7 copy-done.1
  71.5 0.6 copy-done.11
  72.1 14.3 %all_to_all.30 = f32[16,1,128]{2,1,0:T(1,128)S(1)} all-to-all(f32[16,1,128]{2,1,0:T(1,128)S(1)} %get-tuple-element.34), channel_id=1, replica_groups=mesh['gx'=8,'gy'=4,'gz'=16] {'gz'}, dimensions={0} | all-to-all | bytes 16384 | tf_op jit(solution)/shard_map/all_to_all | solution.py:491
  86.4 11.7 %all_to_all.31.sums_ref = f32[32,1,128]{2,1,0:T(1,128)S(1)} all-to-all(f32[32,1,128]{2,1,0:T(1,128)S(1)} %broadcast_in_dim.20), channel_id=1, replica_groups=mesh['gx'=8,'gy'=4,'gz'=16] {'gx','gy'}, dimensions={0} | all-to-all | bytes 32768 | tf_op jit(solution)/shard_map/all_to_all | solution.py:491
  98.1 1.0 copy-done.2
  99.1 0.7 copy-done.21
  99.8 2.6 %shard_map.82 = (f32[8,16,128]{2,1,0:T(8,128)S(1)}, f32[8,16,128]{2,1,0:T(8,128)S(1)}, f32[8,16,128]{2,1,0:T(8,128)S(1)}, f32[16,1,128]{2,1,0:T(1,128)S(1)}, f32...) custom-call(s32[6]{0:T(128)S(1)} %copy-done.21, f32[9,14,24,256]{3,2,1,0:T(8,128)S(1)} %get-tuple-element.31.weights_ref, ...), custom_call_target="tpu_custom_call" | custom-call | tf_op jit(solution)/shard_map/pallas_call | solution.py:470
  102.4 0.6 copy-done.3
  103.0 0.6 copy-done.5
  103.7 0.6 copy-done.13
  104.3 0.6 copy-done.18
  104.9 12.2 %all_to_all.32 = f32[16,1,128]{2,1,0:T(1,128)} all-to-all(f32[16,1,128]{2,1,0:T(1,128)S(1)} %get-tuple-element.38), channel_id=1, replica_groups=mesh['gx'=8,'gy'=4,'gz'=16] {'gz'}, dimensions={0} | all-to-all | bytes 16384 | tf_op jit(solution)/shard_map/all_to_all | solution.py:491
  117.0 1.3 reduce_sum.19
  118.3 0.7 broadcast_in_dim.21
  119.0 11.6 %all_to_all.33.sums_ref = f32[32,1,128]{2,1,0:T(1,128)S(1)} all-to-all(f32[32,1,128]{2,1,0:T(1,128)S(1)} %broadcast_in_dim.21), channel_id=1, replica_groups=mesh['gx'=8,'gy'=4,'gz'=16] {'gx','gy'}, dimensions={0} | all-to-all | bytes 32768 | tf_op jit(solution)/shard_map/all_to_all | solution.py:491
  130.6 0.8 copy-done.4
  131.4 0.8 copy-done.6
  132.3 0.8 copy-done.12
  133.0 0.8 copy-done.14
  133.8 0.7 copy-done.19
  134.5 1.2 shard_map.83
  (39 shorter events, 0.3 us)
Async XLA Ops:
  0.6 0.8 copy-start.7
  1.5 0.8 copy-start.8
  2.3 0.8 copy-start.9
  3.2 0.8 copy-start.10
  4.0 0.7 copy-start.15
  4.6 47.2 %copy-start.17 = (s32[8,4,32]{2,1,0:T(4,128)S(1)}, s32[8,4,32]{2,1,0:T(4,128)}, u32[]{:S(2)}) copy-start(s32[8,4,32]{2,1,0:T(4,128)} %block_ref.1) | copy-start | bytes 12292
  6.7 6.2 %collective-permute-start = (f32[3,3,16,128]{3,2,1,0:T(8,128)S(1)}, f32[3,3,16,128]{3,2,1,0:T(8,128)S(1)}, u32[]{:S(2)}, u32[]{:S(2)}) collective-permute-start(f32[3,3,16,128]{3,2,1,0:T(8,128)S(1)} %get-tuple-element.22), channel_id=1, source_target_pairs={{0,64},{64,128},{128,192},{192,256},{256,320},{320,384},{384,448},... | collective-permute-start | bytes 221192 | tf_op jit(solution)/shard_map/ppermute | solution.py:485
  11.5 5.7 %collective-permute-start.1 = (f32[3,3,16,128]{3,2,1,0:T(8,128)S(1)}, f32[3,3,16,128]{3,2,1,0:T(8,128)S(1)}, u32[]{:S(2)}, u32[]{:S(2)}) collective-permute-start(f32[3,3,16,128]{3,2,1,0:T(8,128)S(1)} %get-tuple-element.24), channel_id=1, source_target_pairs={{64,0},{128,64},{192,128},{256,192},{320,256},{384,320},{448,384},... | collective-permute-start | bytes 221192 | tf_op jit(solution)/shard_map/ppermute | solution.py:486
  17.3 14.8 %collective-permute-start.2 = (f32[3,14,3,128]{3,2,1,0:T(4,128)S(1)}, f32[3,14,3,128]{3,2,1,0:T(4,128)S(1)}, u32[]{:S(2)}, u32[]{:S(2)}) collective-permute-start(f32[3,14,3,128]{3,2,1,0:T(4,128)S(1)} %get-tuple-element.44), channel_id=1, source_target_pairs={{16,0},{32,16},{48,32},{17,1},{33,17},{49,33},{18,2},{34,18},{50,3... | collective-permute-start | bytes 193544 | tf_op jit(solution)/shard_map/ppermute | solution.py:486
  18.6 13.5 %collective-permute-start.3 = (f32[3,14,3,128]{3,2,1,0:T(4,128)S(1)}, f32[3,14,3,128]{3,2,1,0:T(4,128)S(1)}, u32[]{:S(2)}, u32[]{:S(2)}) collective-permute-start(f32[3,14,3,128]{3,2,1,0:T(4,128)S(1)} %get-tuple-element.45), channel_id=1, source_target_pairs={{0,16},{16,32},{32,48},{1,17},{17,33},{33,49},{2,18},{18,34},{34,5... | collective-permute-start | bytes 193544 | tf_op jit(solution)/shard_map/ppermute | solution.py:485
  22.6 16.5 %all-to-all-start = ((f32[16,1,128]{2,1,0:T(1,128)}), f32[16,1,128]{2,1,0:T(1,128)S(1)}, u32[]{:S(2)}, u32[]{:S(2)}) async-start(f32[16,1,128]{2,1,0:T(1,128)} %get-tuple-element.26), calls=%async_computation | async-start | bytes 16384 | tf_op jit(solution)/shard_map/all_to_all | solution.py:491
  32.1 31.6 %copy-start.16 = (f32[6,16]{1,0:T(8,128)S(1)}, f32[6,16]{1,0:T(8,128)}, u32[]{:S(2)}) copy-start(f32[6,16]{1,0:T(8,128)} %table_ref.3) | copy-start | bytes 1156
  32.4 20.4 %collective-permute-start.4 = (f32[3,14,24,3]{3,2,1,0:T(8,128)S(1)}, f32[3,14,24,3]{3,2,1,0:T(8,128)S(1)}, u32[]{:S(2)}, u32[]{:S(2)}) collective-permute-start(f32[3,14,24,3]{3,2,1,0:T(8,128)S(1)} %get-tuple-element.42), channel_id=1, source_target_pairs={{1,0},{2,1},{3,2},{4,3},{5,4},{6,5},{7,6},{8,7},{9,8},{10,9},{11,1... | collective-permute-start | bytes 36296 | tf_op jit(solution)/shard_map/ppermute | solution.py:486
  34.4 18.4 %collective-permute-start.5 = (f32[3,14,24,3]{3,2,1,0:T(8,128)S(1)}, f32[3,14,24,3]{3,2,1,0:T(8,128)S(1)}, u32[]{:S(2)}, u32[]{:S(2)}) collective-permute-start(f32[3,14,24,3]{3,2,1,0:T(8,128)S(1)} %get-tuple-element.43), channel_id=1, source_target_pairs={{0,1},{1,2},{2,3},{3,4},{4,5},{5,6},{6,7},{7,8},{8,9},{9,10},{10,1... | collective-permute-start | bytes 36296 | tf_op jit(solution)/shard_map/ppermute | solution.py:485
  39.8 21.3 %all-to-all-start.1 = ((f32[32,8,128]{2,1,0:T(8,128)}), f32[32,8,128]{2,1,0:T(8,128)S(1)}, u32[]{:S(2)}, u32[]{:S(2)}) async-start(f32[32,8,128]{2,1,0:T(8,128)} %shard_map.79), calls=%async_computation.1 | async-start | bytes 262144 | tf_op jit(solution)/shard_map/all_to_all | solution.py:491
  51.8 46.3 %copy-start.20 = (s32[6]{0:T(128)}, s32[6]{0:T(128)S(1)}, u32[]{:S(2)}) copy-start(s32[6]{0:T(128)S(1)} %stack.36.sides_ref) | copy-start | bytes 76
  63.8 1.2 copy-start
  70.7 0.7 copy-start.1
  71.5 0.6 copy-start.11
  98.1 1.0 copy-start.2
  99.1 0.7 copy-start.21
  102.4 0.6 copy-start.3
  103.0 0.6 copy-start.5
  103.7 0.6 copy-start.13
  104.3 0.6 copy-start.18
  130.6 0.8 copy-start.4
  131.4 0.8 copy-start.6
  132.3 0.8 copy-start.12
  133.0 0.8 copy-start.14
  133.8 0.7 copy-start.19
